TPU v7x, 128 devices: a whole 4x4x4 slice. The times are simulated.
128 devices in a mesh: rows: 32 (over x, z, y_hi), grp: 4 (over y_lo, core).
Axes of the slice: x: 4, y: 4 (y_hi: 2, y_lo: 2; y = y_hi * 2 + y_lo), z: 4, core: 2. Of those that a mesh axis runs over, the one named last changes fastest.
Arguments:
- queries: bfloat16 [8192, 1024], P('rows'), may hold values from -12 to 12
- passages: bfloat16 [32768, 1024], P(('rows', 'grp')), may hold values from -12 to 12
- positive: int32 [8192], P('rows'), may hold values from 0 to 32767
Outputs:
- losses: float32 [8192], P('rows')
- grad_queries: float32 [8192, 1024], P('rows')
- grad_passages: float32 [32768, 1024], P(('rows', 'grp'))
All inputs are finite; a program needn't handle non-finite values.
Results may differ from a plain program's by a relative error of at most 0.0015.
Values may be sent and summed in bfloat16 or wider, within the bound.
A program may use at most 128 MiB of HBM per device.

v0:
```python
import math

import jax
import jax.numpy as jnp
from jax import lax
from jax.sharding import PartitionSpec as P

lowest = -1e30


def from_everyone(value, axis):
    copies = jnp.broadcast_to(value, (lax.axis_size(axis), *value.shape))
    return lax.all_to_all(copies, axis, split_axis=0, concat_axis=0, tiled=True)


def gathered_once(value, axis):
    leaves = jax.tree.leaves(value)
    sequence = sorted(range(len(leaves)), key=lambda k: -leaves[k].size)
    width = (1, *leaves[sequence[0]].shape)[-1]
    lines = [
        jnp.pad(leaves[k].reshape(-1), (0, -leaves[k].size % width)).reshape(-1, width)
        for k in sequence
    ]
    both, at, found = (from_everyone(jnp.concatenate(lines), axis), 0, {})
    for k, line in zip(sequence, lines):
        piece = both[:, at : at + len(line)].reshape(len(both), -1)
        found[k] = piece[:, : leaves[k].size].reshape(-1, *leaves[k].shape)
        at += len(line)
    numbers = iter(range(len(leaves)))
    return jax.tree.map(lambda _: found[next(numbers)], value)


def joined_by_halves(pieces, combine):
    while len(jax.tree.leaves(pieces)[0]) > 1:
        pieces = jax.vmap(combine)(
            *(jax.tree.map(lambda part: part[side::2], pieces) for side in (0, 1))
        )
    return jax.tree.map(lambda part: part[0], pieces)


def joined_all(value, axis, combine):
    pieces = gathered_once(value, axis)
    return joined_by_halves(pieces, combine)


def joined_along(blocks, dim):
    blocks = jnp.moveaxis(blocks, 0, dim)
    dims = blocks.shape
    return blocks.reshape(*dims[:dim], dims[dim] * dims[dim + 1], *dims[dim + 2 :])


def gather_directly(value, axis, dim):
    return joined_along(from_everyone(value, axis), dim)


def taken_together(value, axis):
    return from_everyone(value, axis).sum(axis=0)


def score_block(left_rows, right_rows):
    return lax.dot_general(
        left_rows, right_rows, (((1,), (1,)), ((), ())), preferred_element_type=jnp.float32
    )


def block_size(length):
    return math.gcd(length, 1024)


def combine_parts(first_part, second_part):
    left_max, left_sum, left_pos = first_part
    right_max, right_sum, right_pos = second_part
    joined = jnp.maximum(left_max, right_max)
    merged_sum = left_sum * jnp.exp(left_max - joined) + right_sum * jnp.exp(right_max - joined)
    return (joined, merged_sum, left_pos + right_pos)


def local(queries, passages, positive):
    per_dev = passages.shape[0]
    rows_q = queries.shape[0]
    width = queries.shape[1]
    groups = lax.axis_size("grp")
    group_id = lax.axis_index("grp")
    row_id = lax.axis_index("rows")
    block_id = positive // per_dev
    local_row = positive % per_dev
    share_pos = jnp.where(
        block_id % groups == group_id, block_id // groups * per_dev + local_row, -1
    )
    initial = (
        jnp.full((rows_q,), lowest, jnp.float32),
        jnp.zeros((rows_q,), jnp.float32),
        jnp.zeros((rows_q,), jnp.float32),
    )
    segment = lax.all_gather(passages, "rows", axis=0, tiled=True)
    length = segment.shape[0]
    block_rows = block_size(length)

    def forward_inner_step(block_index, state):
        running_max, running_sum, chosen = state
        first = block_index * block_rows
        sub_block = lax.dynamic_slice_in_dim(segment, first, block_rows, 0)
        scores = score_block(queries, sub_block)
        column = first + lax.iota(jnp.int32, block_rows)
        chosen = chosen + jnp.sum(
            jnp.where(share_pos[:, None] == column[None, :], scores, 0.0), axis=1
        )
        newbest = jnp.maximum(running_max, jnp.max(scores, axis=1))
        running_sum = running_sum * jnp.exp(running_max - newbest) + jnp.sum(
            jnp.exp(scores - newbest[:, None]), axis=1
        )
        return (newbest, running_sum, chosen)

    partial_state = lax.fori_loop(0, length // block_rows, forward_inner_step, initial)
    running_max, running_sum, chosen = joined_all(partial_state, "grp", combine_parts)
    log_total = running_max + jnp.log(running_sum)
    losses = log_total - chosen
    all_lse, all_positive = (
        gather_directly(log_total, "rows", 0),
        gather_directly(positive, "rows", 0),
    )
    own_base = (row_id * groups + group_id) * per_dev
    query_start = jnp.zeros((rows_q, width), jnp.float32)
    passage_start = jnp.zeros((per_dev, width), jnp.float32)
    query_segment = lax.all_gather(passages, "rows", axis=0, tiled=True)
    length = query_segment.shape[0]
    query_block_rows = block_size(length)

    def query_inner_step(block_index, accum):
        first = block_index * query_block_rows
        sub_block = lax.dynamic_slice_in_dim(query_segment, first, query_block_rows, 0)
        scores = score_block(queries, sub_block)
        weights = jnp.exp(scores - log_total[:, None]).astype(jnp.bfloat16)
        accum = accum + jnp.dot(weights, sub_block, preferred_element_type=jnp.float32)
        hit_row = share_pos - first
        inside = (hit_row >= 0) & (hit_row < query_block_rows)
        picked = jnp.take(sub_block, jnp.clip(hit_row, 0, query_block_rows - 1), axis=0).astype(
            jnp.float32
        )
        return accum - jnp.where(inside[:, None], picked, 0.0)

    query_part = lax.fori_loop(0, length // query_block_rows, query_inner_step, query_start)
    passage_segment = lax.all_gather(queries, "rows", axis=0, tiled=True)
    length = passage_segment.shape[0]
    passage_block_rows = block_size(length)

    def passage_inner_step(block_index, accum):
        first = block_index * passage_block_rows
        sub_block = lax.dynamic_slice_in_dim(passage_segment, first, passage_block_rows, 0)
        block_lse = lax.dynamic_slice_in_dim(all_lse, first, passage_block_rows, 0)
        block_pos = lax.dynamic_slice_in_dim(all_positive, first, passage_block_rows, 0)
        scores = score_block(sub_block, passages)
        weights = jnp.exp(scores - block_lse[:, None]).astype(jnp.bfloat16)
        accum = accum + lax.dot_general(
            weights, sub_block, (((0,), (0,)), ((), ())), preferred_element_type=jnp.float32
        )
        hit_row = block_pos - own_base
        inside = (hit_row >= 0) & (hit_row < per_dev)
        target_slot = jnp.where(inside, hit_row, per_dev).astype(jnp.int32)
        return accum.at[target_slot].add(-sub_block.astype(jnp.float32), mode="drop")

    grad_passages = lax.fori_loop(
        0, length // passage_block_rows, passage_inner_step, passage_start
    )
    grad_queries = taken_together(query_part, "grp")
    return (losses, grad_queries, grad_passages)


def solution(mesh):
    placed = (P("rows", None), P(("rows", "grp"), None), P("rows"))
    return jax.shard_map(
        local,
        mesh=mesh,
        in_specs=placed,
        out_specs=(P("rows"), P("rows", None), P(("rows", "grp"), None)),
        check_vma=False,
    )
```

profile of v0, /device:TPU:1, one launch (start us, length us, event | category | flops | bytes accessed | tf_op | source)
XLA Modules:
  0.0 461.5 jit_solution(6739492406988817832)
XLA Ops:
  9.4 158.5 %all-gather.3.cloned.1.call-done = bf16[8192,1024]{1,0:T(8,128)(2,1)} async-done(((bf16[256,1024]{1,0:T(8,128)(2,1)}), bf16[8192,1024]{1,0:T(8,128)(2,1)}) %all-gather.3.cloned.1.call-update) | async-done | bytes 16777232 | tf_op jit(solution)/shard_map/all_gather | solution.py:95
  167.9 22.5 %while.46 = (s32[]{:T(128)}, f32[256]{0:T(256)S(1)}, f32[256]{0:T(256)S(1)}, f32[256]{0:T(256)S(1)}, bf16[8192,1024]{1,0:T(8,128)(2,1)}, /*index=5*/bf16[256,102...) while((s32[]{:T(128)}, f32[256]{0:T(256)S(1)}, ...), condition=%wide.region_4.5_spmd.clone, body=%wide.region_0.4_spmd.clone.sunk | while | flops 538446336 | bytes 4745398 | solution.py:114
  191.0 4.6 all-to-all-start
  199.4 5.4 %all-to-all-start.3 = ((s32[32,1,256]{2,1,0:T(1,128)}), s32[32,1,256]{2,1,0:T(1,128)S(1)}, u32[]{:S(2)}, u32[]{:S(2)}) async-start(s32[32,1,256]{2,1,0:T(1,128)} %broadcast_in_dim.102), calls=%async_computation.3 | async-start | bytes 65536 | tf_op jit(solution)/shard_map/all_to_all | solution.py:13
  205.0 60.2 %while.47 = (s32[]{:T(128)}, f32[256,1024]{1,0:T(8,128)}, bf16[8192,1024]{1,0:T(8,128)(2,1)}, bf16[256,1024]{1,0:T(8,128)(2,1)}, f32[256]{0:T(256)S(1)}, /*index...) while((s32[]{:T(128)}, f32[256,1024]{1,0:T(8,128)}, ...), condition=%wide.region_6.7_spmd.clone, body=%wide.region_5.6_spmd.clone.sunk | while | flops 1075843584 | bytes 12595401 | solution.py:142
  214.4 4.5 fusion.72
  222.0 4.5 fusion.72
  229.7 4.5 fusion.72
  237.2 4.5 fusion.72
  245.4 4.5 fusion.72
  260.6 4.6 fusion.72
  265.9 9.0 %all-to-all-start.2 = ((f32[32,1,256]{2,1,0:T(1,128)}), f32[32,1,256]{2,1,0:T(1,128)S(1)}, u32[]{:S(2)}, u32[]{:S(2)}) async-start(f32[32,1,256]{2,1,0:T(1,128)} %broadcast_in_dim.101), calls=%async_computation.2 | async-start | bytes 65536 | tf_op jit(solution)/shard_map/all_to_all | solution.py:13
  275.5 8.0 %all-to-all-done.2 = f32[32,1,256]{2,1,0:T(1,128)S(1)} async-done(((f32[32,1,256]{2,1,0:T(1,128)}), f32[32,1,256]{2,1,0:T(1,128)S(1)}, u32[]{:S(2)}, u32[]{:S(2)}) %all-to-all-start.2) | async-done | bytes 32800 | tf_op jit(solution)/shard_map/all_to_all | solution.py:13
  287.3 7.8 %all-to-all-start.1 = ((f32[4,256,1024]{2,1,0:T(8,128)}), f32[4,256,1024]{2,1,0:T(8,128)}, u32[]{:S(2)}, u32[]{:S(2)}) async-start(f32[4,256,1024]{2,1,0:T(8,128)} %broadcast_in_dim.100), calls=%async_computation.1 | async-start | bytes 8388608 | tf_op jit(solution)/shard_map/all_to_all | solution.py:13
  295.0 37.8 %all-gather.5.cloned.1.call-done = bf16[8192,1024]{1,0:T(8,128)(2,1)} async-done(((bf16[256,1024]{1,0:T(8,128)(2,1)}), bf16[8192,1024]{1,0:T(8,128)(2,1)}) %all-gather.5.cloned.1.call-update) | async-done | bytes 16777232 | tf_op jit(solution)/shard_map/all_gather | solution.py:143
  333.0 117.7 %while.45 = (s32[]{:T(128)}, f32[256,1024]{1,0:T(8,128)S(1)}, bf16[8192,1024]{1,0:T(8,128)(2,1)}, bf16[256,1024]{1,0:T(8,128)(2,1)S(1)}, f32[8192]{0:T(1024)S(1)...) while((s32[]{:T(128)}, f32[256,1024]{1,0:T(8,128)S(1)}, ...), condition=%wide.region_10.11_spmd, body=%wide.region_8.10_spmd.sunk | while | flops 1077682176 | bytes 9983667 | solution.py:162
  333.0 4.5 fusion.64
  337.6 10.1 %scatter_custom_fusion.5 = f32[256,1024]{1,0:T(8,128)S(1)} fusion(f32[256,1024]{1,0:T(8,128)S(1)} %fusion.64, s32[1024]{0:T(1024)S(1)} %compare_select_fusion.6, bf16[8192,1024]{1,0:T(8,128)(2,1)} %get-tuple-element.696, s32[]{:T(128)S(6)} %select_n.156, s32[]{:T(128)} %constant.189.clone.1..sunk), kind=kCustom, calls=%fused_computation.2.clone.1 | custom fusion | flops 3145728 | bytes 3146244 | tf_op jit(solution)/shard_map/while/body/eval_jaxpr/scatter-add | solution.py:160
  347.7 4.5 fusion.64
  352.3 10.1 %scatter_custom_fusion.5 = f32[256,1024]{1,0:T(8,128)S(1)} fusion(f32[256,1024]{1,0:T(8,128)S(1)} %fusion.64, s32[1024]{0:T(1024)S(1)} %compare_select_fusion.6, bf16[8192,1024]{1,0:T(8,128)(2,1)} %get-tuple-element.696, s32[]{:T(128)S(6)} %select_n.156, s32[]{:T(128)} %constant.189.clone.1..sunk), kind=kCustom, calls=%fused_computation.2.clone.1 | custom fusion | flops 3145728 | bytes 3146244 | tf_op jit(solution)/shard_map/while/body/eval_jaxpr/scatter-add | solution.py:160
  362.4 4.5 fusion.64
  367.0 10.1 %scatter_custom_fusion.5 = f32[256,1024]{1,0:T(8,128)S(1)} fusion(f32[256,1024]{1,0:T(8,128)S(1)} %fusion.64, s32[1024]{0:T(1024)S(1)} %compare_select_fusion.6, bf16[8192,1024]{1,0:T(8,128)(2,1)} %get-tuple-element.696, s32[]{:T(128)S(6)} %select_n.156, s32[]{:T(128)} %constant.189.clone.1..sunk), kind=kCustom, calls=%fused_computation.2.clone.1 | custom fusion | flops 3145728 | bytes 3146244 | tf_op jit(solution)/shard_map/while/body/eval_jaxpr/scatter-add | solution.py:160
  377.1 4.5 fusion.64
  381.7 10.1 %scatter_custom_fusion.5 = f32[256,1024]{1,0:T(8,128)S(1)} fusion(f32[256,1024]{1,0:T(8,128)S(1)} %fusion.64, s32[1024]{0:T(1024)S(1)} %compare_select_fusion.6, bf16[8192,1024]{1,0:T(8,128)(2,1)} %get-tuple-element.696, s32[]{:T(128)S(6)} %select_n.156, s32[]{:T(128)} %constant.189.clone.1..sunk), kind=kCustom, calls=%fused_computation.2.clone.1 | custom fusion | flops 3145728 | bytes 3146244 | tf_op jit(solution)/shard_map/while/body/eval_jaxpr/scatter-add | solution.py:160
  391.9 4.5 fusion.64
  396.4 10.1 %scatter_custom_fusion.5 = f32[256,1024]{1,0:T(8,128)S(1)} fusion(f32[256,1024]{1,0:T(8,128)S(1)} %fusion.64, s32[1024]{0:T(1024)S(1)} %compare_select_fusion.6, bf16[8192,1024]{1,0:T(8,128)(2,1)} %get-tuple-element.696, s32[]{:T(128)S(6)} %select_n.156, s32[]{:T(128)} %constant.189.clone.1..sunk), kind=kCustom, calls=%fused_computation.2.clone.1 | custom fusion | flops 3145728 | bytes 3146244 | tf_op jit(solution)/shard_map/while/body/eval_jaxpr/scatter-add | solution.py:160
  406.6 4.5 fusion.64
  411.1 10.1 %scatter_custom_fusion.5 = f32[256,1024]{1,0:T(8,128)S(1)} fusion(f32[256,1024]{1,0:T(8,128)S(1)} %fusion.64, s32[1024]{0:T(1024)S(1)} %compare_select_fusion.6, bf16[8192,1024]{1,0:T(8,128)(2,1)} %get-tuple-element.696, s32[]{:T(128)S(6)} %select_n.156, s32[]{:T(128)} %constant.189.clone.1..sunk), kind=kCustom, calls=%fused_computation.2.clone.1 | custom fusion | flops 3145728 | bytes 3146244 | tf_op jit(solution)/shard_map/while/body/eval_jaxpr/scatter-add | solution.py:160
  421.3 4.5 fusion.64
  425.9 10.1 %scatter_custom_fusion.5 = f32[256,1024]{1,0:T(8,128)S(1)} fusion(f32[256,1024]{1,0:T(8,128)S(1)} %fusion.64, s32[1024]{0:T(1024)S(1)} %compare_select_fusion.6, bf16[8192,1024]{1,0:T(8,128)(2,1)} %get-tuple-element.696, s32[]{:T(128)S(6)} %select_n.156, s32[]{:T(128)} %constant.189.clone.1..sunk), kind=kCustom, calls=%fused_computation.2.clone.1 | custom fusion | flops 3145728 | bytes 3146244 | tf_op jit(solution)/shard_map/while/body/eval_jaxpr/scatter-add | solution.py:160
  436.0 4.5 fusion.64
  440.6 10.1 %scatter_custom_fusion.5 = f32[256,1024]{1,0:T(8,128)S(1)} fusion(f32[256,1024]{1,0:T(8,128)S(1)} %fusion.64, s32[1024]{0:T(1024)S(1)} %compare_select_fusion.6, bf16[8192,1024]{1,0:T(8,128)(2,1)} %get-tuple-element.696, s32[]{:T(128)S(6)} %select_n.156, s32[]{:T(128)} %constant.189.clone.1..sunk), kind=kCustom, calls=%fused_computation.2.clone.1 | custom fusion | flops 3145728 | bytes 3146244 | tf_op jit(solution)/shard_map/while/body/eval_jaxpr/scatter-add | solution.py:160
  (161 shorter events, 70.9 us)
Async XLA Ops:
  7.2 160.8 %all-gather.3.cloned.1.call-start = ((), (), s32[]{:S(2)}) async-start(), calls=%async_computation.4 | async-start | bytes 17301504 | tf_op jit(solution)/shard_map/all_gather | solution.py:95
  7.9 324.9 %all-gather.5.cloned.1.call-start = ((), (), s32[]{:S(2)}) async-start(), calls=%async_computation.5 | async-start | bytes 17301504 | tf_op jit(solution)/shard_map/all_gather | solution.py:143
  167.9 30.8 %copy-start.3 = (s32[256]{0:T(256)S(1)}, s32[256]{0:T(256)}, u32[]{:S(2)}) copy-start(s32[256]{0:T(256)} %param.11) | copy-start | bytes 3076
  191.0 7.7 %all-to-all-start = ((f32[4,3,256]{2,1,0:T(4,128)}), f32[4,3,256]{2,1,0:T(4,128)S(1)}, u32[]{:S(2)}, u32[]{:S(2)}) async-start(f32[4,3,256]{2,1,0:T(4,128)} %broadcast_in_dim.99), calls=%async_computation | async-start | bytes 32768 | tf_op jit(solution)/shard_map/all_to_all | solution.py:13
  199.4 65.9 %all-to-all-start.3 = ((s32[32,1,256]{2,1,0:T(1,128)}), s32[32,1,256]{2,1,0:T(1,128)S(1)}, u32[]{:S(2)}, u32[]{:S(2)}) async-start(s32[32,1,256]{2,1,0:T(1,128)} %broadcast_in_dim.102), calls=%async_computation.3 | async-start | bytes 65536 | tf_op jit(solution)/shard_map/all_to_all | solution.py:13
  205.0 3.1 copy-start.1
  211.3 3.1 copy-start.1
  218.9 3.1 copy-start.1
  226.6 3.1 copy-start.1
  234.2 3.0 copy-start.1
  241.7 3.7 copy-start.1
  249.9 3.1 copy-start.1
  257.6 3.0 copy-start.1
  265.9 17.6 %all-to-all-start.2 = ((f32[32,1,256]{2,1,0:T(1,128)}), f32[32,1,256]{2,1,0:T(1,128)S(1)}, u32[]{:S(2)}, u32[]{:S(2)}) async-start(f32[32,1,256]{2,1,0:T(1,128)} %broadcast_in_dim.101), calls=%async_computation.2 | async-start | bytes 65536 | tf_op jit(solution)/shard_map/all_to_all | solution.py:13
  287.2 45.7 %copy-start.2 = (bf16[256,1024]{1,0:T(8,128)(2,1)S(1)}, bf16[256,1024]{1,0:T(8,128)(2,1)}, u32[]{:S(2)}) copy-start(bf16[256,1024]{1,0:T(8,128)(2,1)} %param.10) | copy-start | bytes 1572868
  287.3 163.5 %all-to-all-start.1 = ((f32[4,256,1024]{2,1,0:T(8,128)}), f32[4,256,1024]{2,1,0:T(8,128)}, u32[]{:S(2)}, u32[]{:S(2)}) async-start(f32[4,256,1024]{2,1,0:T(8,128)} %broadcast_in_dim.100), calls=%async_computation.1 | async-start | bytes 8388608 | tf_op jit(solution)/shard_map/all_to_all | solution.py:13
  450.7 4.0 copy-start
Sparse Core Ops, SparseCore 0:
  11.2 156.7 all-gather.2
  171.1 161.6 all-gather.4
where the time goes:
time: 466 us; the launch traced here: 462 us
  waiting for transfers between devices  209 us (45%)
  matrix products  91 us (20%)
  other arithmetic  88.7 us (19%)
  local copies, waits for them, and re-layouts  30.8 us (7%)
  starting transfers between devices  26.8 us (6%)
  between operations  14.2 us (3%)
    all_gather x1, waiting for transfers between devices, local(): segment = lax.all_gather(passages, 'rows', axis=0, tiled=True)  159 us
    scatter-add x8, other arithmetic, passage_inner_step(): accum.at[target_slot].add(-sub_block.astype(jnp.float32), mode='drop')  80.8 us
    all_gather x1, waiting for transfers between devices, local(): passage_segment = lax.all_gather(queries, 'rows', axis=0, tiled=True)  37.8 us
    dot_general x8, matrix products, passage_inner_step(): lax.dot_general(weights, sub_block, (((0,), (0,)), ((), ())), preferred_e...  36.3 us
    dot_general x8, matrix products, query_inner_step(): jnp.dot(weights, sub_block, preferred_element_type=jnp.float32)  34.9 us
    all_to_all x4, starting transfers between devices, from_everyone(): return lax.all_to_all(copies, axis, split_axis=0, concat_axis=0, tiled=True)  26.7 us
    dot_general x8, matrix products, score_block(): lax.dot_general(left_rows, right_rows, (((1,), (1,)), ((), ())), preferre...  19.7 us
    dynamic_slice x8, local copies, waits for them, and re-layouts, query_inner_step(): lax.dynamic_slice_in_dim(query_segment, first, query_block_rows, 0)  15.4 us
  transfers between devices with their start and end apart: 6, of which 4 were waited for; matrix products, arithmetic and copies ran while one was open for 45% of the time, Pallas kernels for 0%

commit v1 on v0

v1 whole, which is shorter than its diff:
```python
import jax
import jax.numpy as jnp
from jax import lax
from jax.experimental import pallas as pl
from jax.experimental.pallas import tpu as pltpu
from jax.sharding import PartitionSpec as P

MESH = pl.DeviceIdType.MESH
F32 = jnp.float32
BF16 = jnp.bfloat16
I16 = jnp.int16


def quantized(v):
    most = jnp.maximum(jnp.max(jnp.abs(v), axis=0, keepdims=True), 1e-30)
    return jnp.round(v * (32766.0 / most)).astype(jnp.int32).astype(I16), most * (1.0 / 32766.0)


def restored(v, scale):
    return v.astype(jnp.int32).astype(F32) * scale


def kernel(
    q_ref, p_ref, pos_ref, loss_ref, gq_ref, gp_ref,
    qb, pb, pt, sc, wb, accq, accp, posb, st, stp, stx, stz, lser,
    sx, rq, ys, yss, yr, yrs, bs, bss, br, brs, az, azs, ar, ars, fin, fins, lossb, ssem, rsem,
):
    rows = lax.axis_index("rows")
    grp = lax.axis_index("grp")
    x, z, y_hi = rows // 8, (rows // 2) % 4, rows % 2
    y_lo, c = grp // 2, grp % 2
    y = y_hi * 2 + y_lo
    a = x * (1 - c) + z * c
    b = z * (1 - c) + x * c

    def wrap(v):
        return lax.rem(v + 4, 4)

    def dev(dx, dz, dy, dc):
        return ((dx * 4 + dz) * 2 + dy // 2, (dy % 2) * 2 + dc)

    def dev_ab(da, db):
        return dev(da * (1 - c) + db * c, db * (1 - c) + da * c, y, c)

    def slot(da, db):
        return (da * 4 + db) * (1 - c) + (db * 4 + da) * c

    partner = dev(x, z, y, 1 - c)
    y_pair = dev(x, z, y + 1 - 2 * y_lo, c)
    y_up, y_down = dev(x, z, wrap(y + 1), c), dev(x, z, wrap(y - 1), c)
    a_up, a_down = dev_ab(wrap(a + 1), b), dev_ab(wrap(a - 1), b)
    b_up, b_down = dev_ab(a, wrap(b + 1)), dev_ab(a, wrap(b - 1))
    a1, a2, a3 = wrap(a + 1), wrap(a + 2), wrap(a - 1)
    b1, b2, b3 = wrap(b + 1), wrap(b + 2), wrap(b - 1)
    y_of = [y, wrap(y - 1), wrap(y + 1), wrap(y + 2)]
    x_peers = [dev(wrap(x + d), z, y, c) for d in (1, 2, 3)]
    z_peers = [dev(x, wrap(z + d), y, c) for d in (1, 2, 3)]

    barrier = pltpu.get_barrier_semaphore()
    peers = [partner, y_up, y_down, *x_peers, *z_peers]
    for peer in peers:
        pl.semaphore_signal(barrier, inc=1, device_id=peer, device_id_type=MESH)
    pl.semaphore_wait(barrier, len(peers))

    started, drained = [], set()

    def send(src, dst, device):
        index = len(started)
        copy = pltpu.make_async_remote_copy(
            src_ref=src, dst_ref=dst, send_sem=ssem.at[index], recv_sem=rsem.at[index],
            device_id=device, device_id_type=MESH,
        )
        copy.start()
        started.append(copy)
        return copy

    def drain(copy):
        drained.add(next(k for k, other in enumerate(started) if other is copy))
        copy.wait_send()

    lo, hi = pl.ds(0, 128), pl.ds(128, 128)
    pu0 = send(p_ref.at[lo], pb.at[1, lo], y_up)
    pd0 = send(p_ref.at[hi], pb.at[2, hi], y_down)
    own = q_ref.at[pl.ds((y_lo * 2 + c) * 64, 64)]

    def part(s):
        return qb.at[s, pl.ds(c * 64, 64)]

    def first(s):
        return qb.at[s, pl.ds(c * 64, 32)]

    def second(s):
        return qb.at[s, pl.ds(c * 64 + 32, 32)]

    me = slot(a, b)
    up1 = send(own, part(me), a_up)
    down1 = send(own, part(me), a_down)
    up2 = [send(own, part(me), b_up)]
    down2 = [send(own, part(me), b_down)]
    pu1 = send(p_ref.at[hi], pb.at[1, hi], y_up)
    pd1 = send(p_ref.at[lo], pb.at[2, lo], y_down)
    pos_own = jnp.where(y_lo == 0, pos_ref[0:1, :], pos_ref[1:2, :])
    posb[x, z] = jnp.broadcast_to(pos_own, (8, 128))
    pos_x = [send(posb.at[x, z], posb.at[x, z], peer) for peer in x_peers]
    qb[me] = q_ref[pl.ds(y_lo * 128, 128), :]
    pb[0] = p_ref[...]

    def turn(j):
        for k in range(4):
            pt[k * 256 : (k + 1) * 256, j * 256 : (j + 1) * 256] = pb[
                j, :, k * 256 : (k + 1) * 256
            ].T

    turn(0)

    across = []

    def over(s):
        across.append(send(part(s), part(s), partner))

    def on(s):
        over(s)
        up2.append(send(part(s), part(s), b_up))
        down2.append(send(part(s), part(s), b_down))

    up1.wait_recv()
    fu1 = send(first(slot(a3, b)), first(slot(a3, b)), a_up)
    on(slot(a3, b))
    down1.wait_recv()
    fd1 = send(second(slot(a1, b)), second(slot(a1, b)), a_down)
    on(slot(a1, b))
    for copy in pos_x:
        copy.wait_recv()
    pos_z = [send(posb.at[:, z], posb.at[:, z], peer) for peer in z_peers]
    fu1.wait_recv()
    fd1.wait_recv()
    on(slot(a2, b))

    fu2, fd2 = [], []
    line = [a, a3, a1, a2]

    def along(t):
        up2[t].wait_recv()
        s = slot(line[t], b3)
        fu2.append(send(first(s), first(s), b_up))
        over(s)
        down2[t].wait_recv()
        s = slot(line[t], b1)
        fd2.append(send(second(s), second(s), b_down))
        over(s)

    along(0)
    pu0.wait_recv()
    pfu = send(pb.at[1, lo], pb.at[3, lo], y_up)
    pd0.wait_recv()
    pfd = send(pb.at[2, hi], pb.at[3, hi], y_down)
    for copy in pos_z:
        copy.wait_recv()

    def columns(s):
        return pl.ds(pl.multiple_of(s * 128, 128), 128)

    def mask(s, _):
        where = posb[s // 4, s % 4, 0:1, :]
        for j in range(4):
            base = ((x * 4 + z) * 8 + y_of[j] * 2 + c) * 256
            hit = lax.broadcasted_iota(jnp.int32, (256, 128), 0) == where - base
            wb[j * 256 : (j + 1) * 256, columns(s)] = jnp.where(hit, 1.0, 0.0).astype(BF16)
        return 0

    lax.fori_loop(0, 16, mask, 0)

    def onehot_q(begin, end):
        def step(g, _):
            col = pl.ds(pl.multiple_of(g * 256, 256), 256)
            d = jnp.dot(pt[:, begin:end], wb[begin:end, col], preferred_element_type=F32)
            if begin == 0:
                accq[2 * g], accq[2 * g + 1] = -d[:, :128], -d[:, 128:]
            else:
                accq[2 * g] -= d[:, :128]
                accq[2 * g + 1] -= d[:, 128:]
            return 0

        return step

    def score(begin, end, s1, s2):
        block = pb[begin // 256 : end // 256].reshape(end - begin, 1024)
        both = jnp.concatenate([qb[s1], qb[s2]], axis=0)
        d = lax.dot_general(block, both, (((1,), (1,)), ((), ())), preferred_element_type=F32)
        for s, v in ((s1, d[:, :128]), (s2, d[:, 128:])):
            sc[s, begin:end] = v
            hit = wb[begin:end, columns(s)].astype(F32)
            chosen = jnp.sum(v * hit, axis=0, keepdims=True)
            best = jnp.max(v, axis=0, keepdims=True)
            row = pl.ds(s, 1)
            if begin == 0:
                total = jnp.sum(jnp.exp(v - best), axis=0, keepdims=True)
            else:
                old = st[0, row, :]
                best = jnp.maximum(best, old)
                total = jnp.sum(jnp.exp(v - best), axis=0, keepdims=True)
                total = total + st[1, row, :] * jnp.exp(old - best)
                chosen = chosen + st[2, row, :]
            st[0, row, :], st[1, row, :], st[2, row, :] = best, total, chosen

    def scores(begin, end):
        def step(g, _):
            score(begin, end, 2 * g, 2 * g + 1)
            return 0

        lax.fori_loop(0, 8, step, 0, unroll=2)

    lax.fori_loop(0, 4, onehot_q(0, 256), 0)
    along(1)
    lax.fori_loop(4, 8, onehot_q(0, 256), 0)
    along(2)

    def landed(*indices):
        for k in indices:
            across[k].wait_recv()

    landed(0, 1, 3, 4)
    score(0, 256, slot(a, b3), slot(a, b1))
    score(0, 256, slot(a3, b), slot(a1, b))
    along(3)
    landed(5, 6, 7, 8)
    score(0, 256, slot(a3, b3), slot(a3, b1))
    score(0, 256, slot(a1, b3), slot(a1, b1))
    for t in range(4):
        fu2[t].wait_recv()
        fd2[t].wait_recv()
        over(slot(line[t], b2))
    pu1.wait_recv()
    pd1.wait_recv()
    turn(1)
    turn(2)
    lax.fori_loop(0, 8, onehot_q(256, 768), 0)
    landed(2, 9, 10, 11, 12, 13, 14)
    score(0, 256, slot(a, b), slot(a2, b))
    score(0, 256, slot(a2, b3), slot(a2, b1))
    score(0, 256, slot(a, b2), slot(a3, b2))
    score(0, 256, slot(a1, b2), slot(a2, b2))
    scores(256, 768)
    pfu.wait_recv()
    pfd.wait_recv()
    scores(768, 1024)

    stat = send(st, stp, partner)

    def onehot_p(k, _):
        col = pl.ds(pl.multiple_of(k * 256, 256), 256)
        qk = qb[:, :, col].reshape(2048, 256)
        d = jnp.dot(wb[...], qk, preferred_element_type=F32)
        for j in range(4):
            accp[j, :, col] = -d[j * 256 : (j + 1) * 256]
        return 0

    def join(others):
        best = st[0]
        for other in others:
            best = jnp.maximum(best, other[0])
        total = st[1] * jnp.exp(st[0] - best)
        chosen = st[2]
        for other in others:
            total = total + other[1] * jnp.exp(other[0] - best)
            chosen = chosen + other[2]
        return best, total, chosen

    turn(3)
    lax.fori_loop(0, 8, onehot_q(768, 1024), 0)
    stat.wait_recv()
    drain(stat)
    st[0], st[1], st[2] = join([stp])
    copies = [send(st, stx.at[k], x_peers[k]) for k in range(3)]
    lax.fori_loop(0, 2, onehot_p, 0)
    for copy in copies:
        copy.wait_recv()
        drain(copy)
    st[0], st[1], st[2] = join([stx.at[k] for k in range(3)])
    copies = [send(st, stz.at[k], z_peers[k]) for k in range(3)]
    lax.fori_loop(2, 4, onehot_p, 0)
    for copy in copies:
        copy.wait_recv()
        drain(copy)
    best, total, chosen = join([stz.at[k] for k in range(3)])
    lse = best + jnp.log(total)
    lser[0] = lse
    lser[1] = lse - chosen
    lossb[y_lo] = jnp.broadcast_to(lser[1, pl.ds(x * 4 + z, 1), :], (8, 128))
    loss_copy = send(lossb.at[y_lo], lossb.at[y_lo], y_pair)

    def weigh(s, _):
        wb[:, columns(s)] = jnp.exp(sc[s] - lser[0, pl.ds(s, 1), :]).astype(BF16)
        return 0

    lax.fori_loop(0, 16, weigh, 0)

    def grad_p(begin, end):
        def step(k, _):
            col = pl.ds(pl.multiple_of(k * 256, 256), 256)
            qk = qb[:, :, col].reshape(2048, 256)
            d = jnp.dot(wb[begin:end, :], qk, preferred_element_type=F32)
            for j in range(begin // 256, end // 256):
                accp[j, :, col] += d[j * 256 - begin : (j + 1) * 256 - begin]
            return 0

        lax.fori_loop(0, 4, step, 0)

    mine_d = pl.ds(pl.multiple_of(c * 512, 512), 512)
    other_d = pl.ds(pl.multiple_of((1 - c) * 512, 512), 512)
    top = pl.ds(pl.multiple_of(c * 512, 512), 256)
    bottom = pl.ds(pl.multiple_of(c * 512 + 256, 256), 256)
    halves = (top, bottom)
    a_order, b_order = [a2, a3, a1, a], [b2, b3, b1, b]

    def mine_slots(k):
        return [slot(da, b_order[k]) for da in a_order]

    def other_slots(k):
        return [slot(a_order[k], db) for db in b_order]

    def weights_of(slots):
        return jnp.concatenate([wb[:, columns(s)] for s in slots], axis=1)

    swaps = []

    def grad_q(k):
        slots = other_slots(k)
        d = jnp.dot(pt[other_d, :], weights_of(slots), preferred_element_type=F32)
        for t, s in enumerate(slots):
            sx[k, t] = accq[s, other_d] + d[:, t * 128 : (t + 1) * 128]
        swaps.append(send(sx.at[k], rq.at[k], partner))
        slots = mine_slots(k)
        d = jnp.dot(pt[mine_d, :], weights_of(slots), preferred_element_type=F32)
        for t, s in enumerate(slots):
            accq[s, mine_d] += d[:, t * 128 : (t + 1) * 128]

    def swapped(k):
        swaps[k].wait_recv()
        for t, s in enumerate(mine_slots(k)):
            accq[s, mine_d] += rq[k, t]

    def hop_p(n, j, half, device):
        v, scale = quantized(accp[j, half])
        ys[n] = v
        for k in range(8):
            yss[n, k : k + 1, :] = scale[:, k * 128 : (k + 1) * 128]
        return send(ys.at[n], yr.at[n], device), send(yss.at[n], yrs.at[n], device)

    def arrive_p(n, hop):
        for copy in hop:
            copy.wait_recv()
        scale = jnp.concatenate([yrs[n, k : k + 1, :] for k in range(8)], axis=1)
        return restored(yr[n], scale)

    def hop_b(n, k, side, device):
        for t, s in enumerate(mine_slots(k)):
            bs[n, t], scale = quantized(accq[s, halves[side]])
            bss[n, t : t + 1, :] = scale
        return send(bs.at[n], br.at[n], device), send(bss.at[n], brs.at[n], device)

    def arrive_b(n, hop, k, side):
        for copy in hop:
            copy.wait_recv()
        for t, s in enumerate(mine_slots(k)):
            accq[s, halves[side]] += restored(br[n, t], brs[n, t : t + 1, :])

    def hop_a(n, da, side, device):
        az[n], scale = quantized(accq[slot(da, b), halves[side]])
        azs[n, 0:1, :] = scale
        return send(az.at[n], ar.at[n], device), send(azs.at[n], ars.at[n], device)

    def arrive_a(n, hop, da, side):
        for copy in hop:
            copy.wait_recv()
        accq[slot(da, b), halves[side]] += restored(ar[n], ars[n, 0:1, :])

    grad_q(0)
    grad_p(768, 1024)
    pu_a = hop_p(0, 3, lo, y_up)
    pd_a = hop_p(1, 3, hi, y_down)
    swapped(0)
    qu_a = hop_b(0, 0, 0, b_up)
    qd_a = hop_b(1, 0, 1, b_down)
    grad_q(1)
    grad_q(2)
    swapped(1)
    qd_b = hop_b(2, 1, 0, b_down)
    swapped(2)
    qu_b = hop_b(3, 2, 1, b_up)
    grad_q(3)
    arrive_b(0, qu_a, 2, 0)
    qu_c = hop_b(4, 2, 0, b_up)
    arrive_b(1, qd_a, 1, 1)
    qd_c = hop_b(5, 1, 1, b_down)
    grad_p(256, 768)
    pu_b = hop_p(2, 2, hi, y_up)
    pd_b = hop_p(3, 1, lo, y_down)
    accp[2, lo] += arrive_p(0, pu_a)
    pu_c = hop_p(4, 2, lo, y_up)
    accp[1, hi] += arrive_p(1, pd_a)
    pd_c = hop_p(5, 1, hi, y_down)
    swapped(3)
    arrive_b(2, qd_b, 3, 0)
    arrive_b(3, qu_b, 3, 1)
    arrive_b(4, qu_c, 3, 0)
    arrive_b(5, qd_c, 3, 1)
    vu_a = hop_a(0, a2, 0, a_up)
    vd_a = hop_a(1, a2, 1, a_down)
    vd_b = hop_a(2, a3, 0, a_down)
    vu_b = hop_a(3, a1, 1, a_up)
    grad_p(0, 256)
    arrive_a(0, vu_a, a1, 0)
    vu_c = hop_a(4, a1, 0, a_up)
    arrive_a(1, vd_a, a3, 1)
    vd_c = hop_a(5, a3, 1, a_down)
    arrive_a(2, vd_b, a, 0)
    arrive_a(3, vu_b, a, 1)
    arrive_a(4, vu_c, a, 0)
    arrive_a(5, vd_c, a, 1)

    fin[y_lo, c], scale = quantized(accq[me, mine_d].T)
    for k in range(4):
        fins[y_lo, c, k : k + 1, :] = scale[:, k * 128 : (k + 1) * 128]

    def share(h, device):
        return [send(f.at[h, c], f.at[h, c], device) for f in (fin, fins)]

    out1 = share(y_lo, y_pair)
    out2 = share(y_lo, partner)
    gp_ref[lo, :] = accp[0, lo] + arrive_p(3, pd_b) + arrive_p(4, pu_c)
    gp_ref[hi, :] = accp[0, hi] + arrive_p(2, pu_b) + arrive_p(5, pd_c)
    loss_copy.wait_recv()
    loss_ref[0:1, :] = lossb[0, 0:1, :]
    loss_ref[1:2, :] = lossb[1, 0:1, :]
    for copy in out1:
        copy.wait_recv()
    out3 = share(1 - y_lo, partner)

    def finish(h, core):
        scale = jnp.concatenate([fins[h, core, k : k + 1, :] for k in range(4)], axis=1)
        gq_ref[pl.ds(pl.multiple_of(h * 128, 128), 128), pl.ds(pl.multiple_of(core * 512, 512), 512)] = (
            restored(fin[h, core], scale)
        )

    finish(y_lo, c)
    finish(1 - y_lo, c)
    for copy in out2:
        copy.wait_recv()
    finish(y_lo, 1 - c)
    for copy in out3:
        copy.wait_recv()
    finish(1 - y_lo, 1 - c)
    for k, copy in enumerate(started):
        if k not in drained:
            copy.wait_send()


def local(queries, passages, positive):
    vmem = pltpu.VMEM
    space = pl.BlockSpec(memory_space=vmem)
    loss, gq, gp = pl.pallas_call(
        kernel,
        out_shape=(
            jax.ShapeDtypeStruct((2, 128), F32),
            jax.ShapeDtypeStruct((256, 1024), F32),
            jax.ShapeDtypeStruct((256, 1024), F32),
        ),
        in_specs=[space] * 3,
        out_specs=(space,) * 3,
        scratch_shapes=[
            vmem((16, 128, 1024), BF16),
            vmem((4, 256, 1024), BF16),
            vmem((1024, 1024), BF16),
            vmem((16, 1024, 128), F32),
            vmem((1024, 2048), BF16),
            vmem((16, 1024, 128), F32),
            vmem((4, 256, 1024), F32),
            vmem((4, 4, 8, 128), jnp.int32),
            vmem((3, 16, 128), F32),
            vmem((3, 16, 128), F32),
            vmem((3, 3, 16, 128), F32),
            vmem((3, 3, 16, 128), F32),
            vmem((2, 16, 128), F32),
            vmem((4, 4, 512, 128), F32),
            vmem((4, 4, 512, 128), F32),
            vmem((6, 128, 1024), I16),
            vmem((6, 8, 128), F32),
            vmem((6, 128, 1024), I16),
            vmem((6, 8, 128), F32),
            vmem((6, 4, 256, 128), I16),
            vmem((6, 4, 128), F32),
            vmem((6, 4, 256, 128), I16),
            vmem((6, 4, 128), F32),
            vmem((6, 256, 128), I16),
            vmem((6, 1, 128), F32),
            vmem((6, 256, 128), I16),
            vmem((6, 1, 128), F32),
            vmem((2, 2, 128, 512), I16),
            vmem((2, 2, 4, 128), F32),
            vmem((2, 8, 128), F32),
            pltpu.SemaphoreType.DMA((128,)),
            pltpu.SemaphoreType.DMA((128,)),
        ],
        compiler_params=pltpu.CompilerParams(
            collective_id=0, has_side_effects=True, vmem_limit_bytes=66_000_000
        ),
    )(queries, passages, positive.reshape(2, 128))
    return loss.reshape(256), gq, gp


def solution(mesh):
    placed = (P("rows", None), P(("rows", "grp"), None), P("rows"))
    return jax.shard_map(
        local,
        mesh=mesh,
        in_specs=placed,
        out_specs=(P("rows"), P("rows", None), P(("rows", "grp"), None)),
        check_vma=False,
    )
```

time: 466 us -> 90.4 us (0.19)
  waiting for transfers between devices: 209 us -> 0 us
  matrix products: 91 us -> 0 us
  other arithmetic: 88.7 us -> 0 us
  Pallas kernels: 0 us -> 85.1 us
  starting transfers between devices: 26.8 us -> 0 us
  local copies, waits for them, and re-layouts: 30.8 us -> 4.53 us
  between operations: 14.2 us -> 0.65 us
    all_gather x2 -> x0, waiting for transfers between devices: 196 us -> none  [the longest x1 159 us: local(): segment = lax.all_gather(passages, 'rows', axis=0, tiled=True)]
    dot_general x24 -> x0, matrix products: 91 us -> none  [the longest x8 36.3 us: passage_inner_step(): lax.dot_general(weights, sub_block, (((0,), (0,)), ((), ())), preferred_e...]
    pallas_call x0 -> x1, Pallas kernels: none -> 85.1 us  [local(): pl.pallas_call(kernel, out_shape=(jax.ShapeDtypeStruct((2, 128), F32), ja...]
    scatter-add x8 -> x0, other arithmetic: 80.8 us -> none  [passage_inner_step(): accum.at[target_slot].add(-sub_block.astype(jnp.float32), mode='drop')]
    all_to_all x4 -> x0, starting transfers between devices: 26.7 us -> none  [from_everyone(): return lax.all_to_all(copies, axis, split_axis=0, concat_axis=0, tiled=True)]
    dynamic_slice x16 -> x0, local copies, waits for them, and re-layouts: 15.5 us -> none  [the longest x8 15.4 us: query_inner_step(): lax.dynamic_slice_in_dim(query_segment, first, query_block_rows, 0)]
    all_to_all x4 -> x0, waiting for transfers between devices: 11.2 us -> none  [from_everyone(): return lax.all_to_all(copies, axis, split_axis=0, concat_axis=0, tiled=True)]
    gather x8 -> x0, local copies, waits for them, and re-layouts: 9.35 us -> none  [query_inner_step(): jnp.take(sub_block, jnp.clip(hit_row, 0, query_block_rows - 1), axis=0)]
  transfers between devices with their start and end apart: 6 -> 0, of which waited for: 4 -> 0; matrix products, arithmetic and copies ran while one was open for 45% -> 0% of each run, Pallas kernels for 0% -> 0%
where the time goes in v1:
time: 90.4 us; the launch traced here: 90.3 us
  Pallas kernels  85.1 us (94%)
  local copies, waits for them, and re-layouts  4.53 us (5%)
    pallas_call x1, Pallas kernels, local(): pl.pallas_call(kernel, out_shape=(jax.ShapeDtypeStruct((2, 128), F32), ja...  85.1 us
    unnamed x7, local copies, waits for them, and re-layouts  4.53 us

profile of v1, /device:TPU:1, one launch (start us, length us, event | category | flops | bytes accessed | tf_op | source)
XLA Modules:
  0.0 90.3 jit_solution(15229219449178086287)
XLA Ops:
  0.6 85.1 %shard_map.58 = (f32[2,128]{1,0:T(2,128)}, f32[256,1024]{1,0:T(8,128)}, f32[256,1024]{1,0:T(8,128)}) custom-call(bf16[256,1024]{1,0:T(8,128)(2,1)} %q_ref.1, bf16[256,1024]{1,0:T(8,128)(2,1)} %p_ref.1, s32[2,128]{1,0:T(2,128)} %bitcast.2), custom_call_target="tpu_custom_call" | custom-call | tf_op jit(solution)/shard_map/pallas_call | solution.py:462
  85.7 0.0 copy-start.1
  85.7 0.6 copy-done.1
  86.3 0.6 copy.9
  86.9 0.0 copy-start
  86.9 2.4 %copy.10 = f32[256,1024]{1,0:T(8,128)} copy(f32[256,1024]{1,0:T(8,128)} %get-tuple-element.13) | data formatting | bytes 2097152
  89.3 0.0 copy-done
  89.3 1.0 %copy.11 = f32[256,1024]{1,0:T(8,128)} copy(f32[256,1024]{1,0:T(8,128)S(1)} %copy-done) | data formatting | bytes 2097152
Async XLA Ops:
  85.7 0.6 copy-start.1
  86.9 2.4 %copy-start = (f32[256,1024]{1,0:T(8,128)S(1)}, f32[256,1024]{1,0:T(8,128)}, u32[]{:S(2)}) copy-start(f32[256,1024]{1,0:T(8,128)} %get-tuple-element.14) | copy-start | bytes 3145732

commit v2 on v1

--- a/solution.py
+++ b/solution.py
@@ -22,8 +22,8 @@
 
 def kernel(
     q_ref, p_ref, pos_ref, loss_ref, gq_ref, gp_ref,
-    qb, pb, pt, sc, wb, accq, accp, posb, st, stp, stx, stz, lser,
-    sx, rq, ys, yss, yr, yrs, bs, bss, br, brs, az, azs, ar, ars, fin, fins, lossb, ssem, rsem,
+    qb, pb, pt, sc, wb, wq, accq, accp, posb, st, stp, stx, stz, lser,
+    sx, rq, ys, yss, yr, yrs, bs, bss, br, brs, az, azs, ar, ars, fin, fins, lossb, lsem, ssem, rsem,
 ):
     rows = lax.axis_index("rows")
     grp = lax.axis_index("grp")
@@ -60,7 +60,16 @@
     peers = [partner, y_up, y_down, *x_peers, *z_peers]
     for peer in peers:
         pl.semaphore_signal(barrier, inc=1, device_id=peer, device_id_type=MESH)
+    me = slot(a, b)
+    fetches = [
+        pltpu.make_async_copy(p_ref, pb.at[0], lsem.at[0]),
+        pltpu.make_async_copy(q_ref.at[pl.ds(y_lo * 128, 128)], qb.at[me], lsem.at[1]),
+    ]
+    for fetch in fetches:
+        fetch.start()
     pl.semaphore_wait(barrier, len(peers))
+    for fetch in fetches:
+        fetch.wait()
 
     started, drained = [], set()
 
@@ -79,9 +88,8 @@
         copy.wait_send()
 
     lo, hi = pl.ds(0, 128), pl.ds(128, 128)
-    pu0 = send(p_ref.at[lo], pb.at[1, lo], y_up)
-    pd0 = send(p_ref.at[hi], pb.at[2, hi], y_down)
-    own = q_ref.at[pl.ds((y_lo * 2 + c) * 64, 64)]
+    pu0 = send(pb.at[0, lo], pb.at[1, lo], y_up)
+    pd0 = send(pb.at[0, hi], pb.at[2, hi], y_down)
 
     def part(s):
         return qb.at[s, pl.ds(c * 64, 64)]
@@ -92,18 +100,16 @@
     def second(s):
         return qb.at[s, pl.ds(c * 64 + 32, 32)]
 
-    me = slot(a, b)
+    own = part(me)
     up1 = send(own, part(me), a_up)
     down1 = send(own, part(me), a_down)
     up2 = [send(own, part(me), b_up)]
     down2 = [send(own, part(me), b_down)]
-    pu1 = send(p_ref.at[hi], pb.at[1, hi], y_up)
-    pd1 = send(p_ref.at[lo], pb.at[2, lo], y_down)
+    pu1 = send(pb.at[0, hi], pb.at[1, hi], y_up)
+    pd1 = send(pb.at[0, lo], pb.at[2, lo], y_down)
     pos_own = jnp.where(y_lo == 0, pos_ref[0:1, :], pos_ref[1:2, :])
     posb[x, z] = jnp.broadcast_to(pos_own, (8, 128))
     pos_x = [send(posb.at[x, z], posb.at[x, z], peer) for peer in x_peers]
-    qb[me] = q_ref[pl.ds(y_lo * 128, 128), :]
-    pb[0] = p_ref[...]
 
     def turn(j):
         for k in range(4):
@@ -170,25 +176,15 @@
 
     lax.fori_loop(0, 16, mask, 0)
 
-    def onehot_q(begin, end):
-        def step(g, _):
-            col = pl.ds(pl.multiple_of(g * 256, 256), 256)
-            d = jnp.dot(pt[:, begin:end], wb[begin:end, col], preferred_element_type=F32)
-            if begin == 0:
-                accq[2 * g], accq[2 * g + 1] = -d[:, :128], -d[:, 128:]
-            else:
-                accq[2 * g] -= d[:, :128]
-                accq[2 * g + 1] -= d[:, 128:]
-            return 0
-
-        return step
-
-    def score(begin, end, s1, s2):
+    def product(begin, end, s1, s2):
         block = pb[begin // 256 : end // 256].reshape(end - begin, 1024)
         both = jnp.concatenate([qb[s1], qb[s2]], axis=0)
         d = lax.dot_general(block, both, (((1,), (1,)), ((), ())), preferred_element_type=F32)
-        for s, v in ((s1, d[:, :128]), (s2, d[:, 128:])):
-            sc[s, begin:end] = v
+        sc[s1, begin:end], sc[s2, begin:end] = d[:, :128], d[:, 128:]
+
+    def statistics(begin, end, s1, s2):
+        for s in (s1, s2):
+            v = sc[s, begin:end]
             hit = wb[begin:end, columns(s)].astype(F32)
             chosen = jnp.sum(v * hit, axis=0, keepdims=True)
             best = jnp.max(v, axis=0, keepdims=True)
@@ -203,29 +199,36 @@
                 chosen = chosen + st[2, row, :]
             st[0, row, :], st[1, row, :], st[2, row, :] = best, total, chosen
 
-    def scores(begin, end):
-        def step(g, _):
-            score(begin, end, 2 * g, 2 * g + 1)
-            return 0
-
-        lax.fori_loop(0, 8, step, 0, unroll=2)
-
-    lax.fori_loop(0, 4, onehot_q(0, 256), 0)
-    along(1)
-    lax.fori_loop(4, 8, onehot_q(0, 256), 0)
-    along(2)
+    def score(*items):
+        for k, item in enumerate(items):
+            if k:
+                statistics(*items[k - 1])
+            product(*item)
+        statistics(*items[-1])
 
     def landed(*indices):
         for k in indices:
             across[k].wait_recv()
 
+    along(1)
+    along(2)
+    early = [
+        (slot(a, b3), slot(a, b1)),
+        (slot(a3, b), slot(a1, b)),
+        (slot(a3, b3), slot(a3, b1)),
+        (slot(a1, b3), slot(a1, b1)),
+    ]
+    late = [
+        (slot(a, b), slot(a2, b)),
+        (slot(a2, b3), slot(a2, b1)),
+        (slot(a, b2), slot(a3, b2)),
+        (slot(a1, b2), slot(a2, b2)),
+    ]
     landed(0, 1, 3, 4)
-    score(0, 256, slot(a, b3), slot(a, b1))
-    score(0, 256, slot(a3, b), slot(a1, b))
+    score((0, 256, *early[0]), (0, 256, *early[1]))
     along(3)
     landed(5, 6, 7, 8)
-    score(0, 256, slot(a3, b3), slot(a3, b1))
-    score(0, 256, slot(a1, b3), slot(a1, b1))
+    score((0, 256, *early[2]), (0, 256, *early[3]))
     for t in range(4):
         fu2[t].wait_recv()
         fd2[t].wait_recv()
@@ -234,16 +237,12 @@
     pd1.wait_recv()
     turn(1)
     turn(2)
-    lax.fori_loop(0, 8, onehot_q(256, 768), 0)
+    score(*[(256, 768, *pair) for pair in early])
     landed(2, 9, 10, 11, 12, 13, 14)
-    score(0, 256, slot(a, b), slot(a2, b))
-    score(0, 256, slot(a2, b3), slot(a2, b1))
-    score(0, 256, slot(a, b2), slot(a3, b2))
-    score(0, 256, slot(a1, b2), slot(a2, b2))
-    scores(256, 768)
+    score(*[(0, 768, *pair) for pair in late])
     pfu.wait_recv()
     pfd.wait_recv()
-    scores(768, 1024)
+    score(*[(768, 1024, 2 * g, 2 * g + 1) for g in range(8)])
 
     stat = send(st, stp, partner)
 
@@ -266,19 +265,19 @@
             chosen = chosen + other[2]
         return best, total, chosen
 
+    lax.fori_loop(0, 1, onehot_p, 0)
     turn(3)
-    lax.fori_loop(0, 8, onehot_q(768, 1024), 0)
     stat.wait_recv()
     drain(stat)
     st[0], st[1], st[2] = join([stp])
     copies = [send(st, stx.at[k], x_peers[k]) for k in range(3)]
-    lax.fori_loop(0, 2, onehot_p, 0)
+    lax.fori_loop(1, 3, onehot_p, 0)
     for copy in copies:
         copy.wait_recv()
         drain(copy)
     st[0], st[1], st[2] = join([stx.at[k] for k in range(3)])
     copies = [send(st, stz.at[k], z_peers[k]) for k in range(3)]
-    lax.fori_loop(2, 4, onehot_p, 0)
+    lax.fori_loop(3, 4, onehot_p, 0)
     for copy in copies:
         copy.wait_recv()
         drain(copy)
@@ -286,31 +285,37 @@
     lse = best + jnp.log(total)
     lser[0] = lse
     lser[1] = lse - chosen
+    v = jnp.exp(chosen - lse) - 1.0
+    exact = v.astype(BF16).astype(F32)
+    plain = (v == 0.0) | (exact == 0.0)
+    lser[2] = jnp.where(plain, 1.0, exact / jnp.where(plain, 1.0, v))
+    lser[3] = jnp.where(plain, 1.0, v / jnp.where(plain, 1.0, exact))
     lossb[y_lo] = jnp.broadcast_to(lser[1, pl.ds(x * 4 + z, 1), :], (8, 128))
     loss_copy = send(lossb.at[y_lo], lossb.at[y_lo], y_pair)
 
     def weigh(s, _):
-        wb[:, columns(s)] = jnp.exp(sc[s] - lser[0, pl.ds(s, 1), :]).astype(BF16)
+        w = jnp.exp(sc[s] - lser[0, pl.ds(s, 1), :])
+        less = (w - wb[:, columns(s)].astype(F32)) * lser[2, pl.ds(s, 1), :]
+        wb[:, columns(s)] = w.astype(BF16)
+        wq[:, columns(s)] = less.astype(BF16)
         return 0
 
     lax.fori_loop(0, 16, weigh, 0)
 
-    def grad_p(begin, end):
+    def grad_p(h):
         def step(k, _):
             col = pl.ds(pl.multiple_of(k * 256, 256), 256)
             qk = qb[:, :, col].reshape(2048, 256)
-            d = jnp.dot(wb[begin:end, :], qk, preferred_element_type=F32)
-            for j in range(begin // 256, end // 256):
-                accp[j, :, col] += d[j * 256 - begin : (j + 1) * 256 - begin]
+            d = jnp.dot(wb[...], qk, preferred_element_type=F32)
+            for j in range(4):
+                accp[j, :, col] += d[j * 256 : (j + 1) * 256]
             return 0
 
-        lax.fori_loop(0, 4, step, 0)
+        lax.fori_loop(2 * h, 2 * h + 2, step, 0)
 
     mine_d = pl.ds(pl.multiple_of(c * 512, 512), 512)
     other_d = pl.ds(pl.multiple_of((1 - c) * 512, 512), 512)
-    top = pl.ds(pl.multiple_of(c * 512, 512), 256)
-    bottom = pl.ds(pl.multiple_of(c * 512 + 256, 256), 256)
-    halves = (top, bottom)
+    halves = (pl.ds(0, 256), pl.ds(256, 256))
     a_order, b_order = [a2, a3, a1, a], [b2, b3, b1, b]
 
     def mine_slots(k):
@@ -320,38 +325,58 @@
         return [slot(a_order[k], db) for db in b_order]
 
     def weights_of(slots):
-        return jnp.concatenate([wb[:, columns(s)] for s in slots], axis=1)
+        return jnp.concatenate([wq[:, columns(s)] for s in slots], axis=1)
 
     swaps = []
 
     def grad_q(k):
         slots = other_slots(k)
         d = jnp.dot(pt[other_d, :], weights_of(slots), preferred_element_type=F32)
-        for t, s in enumerate(slots):
-            sx[k, t] = accq[s, other_d] + d[:, t * 128 : (t + 1) * 128]
+        for t in range(4):
+            sx[k, t] = d[:, t * 128 : (t + 1) * 128]
         swaps.append(send(sx.at[k], rq.at[k], partner))
         slots = mine_slots(k)
         d = jnp.dot(pt[mine_d, :], weights_of(slots), preferred_element_type=F32)
         for t, s in enumerate(slots):
-            accq[s, mine_d] += d[:, t * 128 : (t + 1) * 128]
+            accq[s] = d[:, t * 128 : (t + 1) * 128]
 
     def swapped(k):
         swaps[k].wait_recv()
         for t, s in enumerate(mine_slots(k)):
-            accq[s, mine_d] += rq[k, t]
-
-    def hop_p(n, j, half, device):
-        v, scale = quantized(accp[j, half])
-        ys[n] = v
-        for k in range(8):
-            yss[n, k : k + 1, :] = scale[:, k * 128 : (k + 1) * 128]
-        return send(ys.at[n], yr.at[n], device), send(yss.at[n], yrs.at[n], device)
-
-    def arrive_p(n, hop):
+            accq[s] += rq[k, t]
+
+    def hop_p(h, n, j, half, device):
+        v, scale = quantized(accp[j, half, h * 512 : (h + 1) * 512])
+        ys[h, n] = v
+        for k in range(4):
+            yss[h, n, k : k + 1, :] = scale[:, k * 128 : (k + 1) * 128]
+        return send(ys.at[h, n], yr.at[h, n], device), send(yss.at[h, n], yrs.at[h, n], device)
+
+    def arrive_p(h, n, hop):
         for copy in hop:
             copy.wait_recv()
-        scale = jnp.concatenate([yrs[n, k : k + 1, :] for k in range(8)], axis=1)
-        return restored(yr[n], scale)
+        scale = jnp.concatenate([yrs[h, n, k : k + 1, :] for k in range(4)], axis=1)
+        return restored(yr[h, n], scale)
+
+    hops_p = {}
+
+    def begin_p(h):
+        hops_p[h, 0] = hop_p(h, 0, 3, lo, y_up)
+        hops_p[h, 1] = hop_p(h, 1, 3, hi, y_down)
+        hops_p[h, 2] = hop_p(h, 2, 2, hi, y_up)
+        hops_p[h, 3] = hop_p(h, 3, 1, lo, y_down)
+
+    def relay_p(h):
+        part = pl.ds(h * 512, 512)
+        accp[2, lo, part] += arrive_p(h, 0, hops_p[h, 0])
+        hops_p[h, 4] = hop_p(h, 4, 2, lo, y_up)
+        accp[1, hi, part] += arrive_p(h, 1, hops_p[h, 1])
+        hops_p[h, 5] = hop_p(h, 5, 1, hi, y_down)
+
+    def end_p(h):
+        part = pl.ds(h * 512, 512)
+        gp_ref[lo, part] = accp[0, lo, part] + arrive_p(h, 3, hops_p[h, 3]) + arrive_p(h, 4, hops_p[h, 4])
+        gp_ref[hi, part] = accp[0, hi, part] + arrive_p(h, 2, hops_p[h, 2]) + arrive_p(h, 5, hops_p[h, 5])
 
     def hop_b(n, k, side, device):
         for t, s in enumerate(mine_slots(k)):
@@ -376,16 +401,15 @@
         accq[slot(da, b), halves[side]] += restored(ar[n], ars[n, 0:1, :])
 
     grad_q(0)
-    grad_p(768, 1024)
-    pu_a = hop_p(0, 3, lo, y_up)
-    pd_a = hop_p(1, 3, hi, y_down)
+    grad_q(1)
     swapped(0)
     qu_a = hop_b(0, 0, 0, b_up)
     qd_a = hop_b(1, 0, 1, b_down)
-    grad_q(1)
     grad_q(2)
     swapped(1)
     qd_b = hop_b(2, 1, 0, b_down)
+    grad_p(0)
+    begin_p(0)
     swapped(2)
     qu_b = hop_b(3, 2, 1, b_up)
     grad_q(3)
@@ -393,13 +417,9 @@
     qu_c = hop_b(4, 2, 0, b_up)
     arrive_b(1, qd_a, 1, 1)
     qd_c = hop_b(5, 1, 1, b_down)
-    grad_p(256, 768)
-    pu_b = hop_p(2, 2, hi, y_up)
-    pd_b = hop_p(3, 1, lo, y_down)
-    accp[2, lo] += arrive_p(0, pu_a)
-    pu_c = hop_p(4, 2, lo, y_up)
-    accp[1, hi] += arrive_p(1, pd_a)
-    pd_c = hop_p(5, 1, hi, y_down)
+    grad_p(1)
+    begin_p(1)
+    relay_p(0)
     swapped(3)
     arrive_b(2, qd_b, 3, 0)
     arrive_b(3, qu_b, 3, 1)
@@ -409,7 +429,7 @@
     vd_a = hop_a(1, a2, 1, a_down)
     vd_b = hop_a(2, a3, 0, a_down)
     vu_b = hop_a(3, a1, 1, a_up)
-    grad_p(0, 256)
+    relay_p(1)
     arrive_a(0, vu_a, a1, 0)
     vu_c = hop_a(4, a1, 0, a_up)
     arrive_a(1, vd_a, a3, 1)
@@ -419,7 +439,7 @@
     arrive_a(4, vu_c, a, 0)
     arrive_a(5, vd_c, a, 1)
 
-    fin[y_lo, c], scale = quantized(accq[me, mine_d].T)
+    fin[y_lo, c], scale = quantized((accq[me] * lser[3, pl.ds(x * 4 + z, 1), :]).T)
     for k in range(4):
         fins[y_lo, c, k : k + 1, :] = scale[:, k * 128 : (k + 1) * 128]
 
@@ -428,8 +448,8 @@
 
     out1 = share(y_lo, y_pair)
     out2 = share(y_lo, partner)
-    gp_ref[lo, :] = accp[0, lo] + arrive_p(3, pd_b) + arrive_p(4, pu_c)
-    gp_ref[hi, :] = accp[0, hi] + arrive_p(2, pu_b) + arrive_p(5, pd_c)
+    end_p(0)
+    end_p(1)
     loss_copy.wait_recv()
     loss_ref[0:1, :] = lossb[0, 0:1, :]
     loss_ref[1:2, :] = lossb[1, 0:1, :]
@@ -466,7 +486,7 @@
             jax.ShapeDtypeStruct((256, 1024), F32),
             jax.ShapeDtypeStruct((256, 1024), F32),
         ),
-        in_specs=[space] * 3,
+        in_specs=[pl.BlockSpec(memory_space=pl.ANY)] * 2 + [space],
         out_specs=(space,) * 3,
         scratch_shapes=[
             vmem((16, 128, 1024), BF16),
@@ -474,20 +494,21 @@
             vmem((1024, 1024), BF16),
             vmem((16, 1024, 128), F32),
             vmem((1024, 2048), BF16),
-            vmem((16, 1024, 128), F32),
+            vmem((1024, 2048), BF16),
+            vmem((16, 512, 128), F32),
             vmem((4, 256, 1024), F32),
             vmem((4, 4, 8, 128), jnp.int32),
             vmem((3, 16, 128), F32),
             vmem((3, 16, 128), F32),
             vmem((3, 3, 16, 128), F32),
             vmem((3, 3, 16, 128), F32),
-            vmem((2, 16, 128), F32),
+            vmem((4, 16, 128), F32),
             vmem((4, 4, 512, 128), F32),
             vmem((4, 4, 512, 128), F32),
-            vmem((6, 128, 1024), I16),
-            vmem((6, 8, 128), F32),
-            vmem((6, 128, 1024), I16),
-            vmem((6, 8, 128), F32),
+            vmem((2, 6, 128, 512), I16),
+            vmem((2, 6, 4, 128), F32),
+            vmem((2, 6, 128, 512), I16),
+            vmem((2, 6, 4, 128), F32),
             vmem((6, 4, 256, 128), I16),
             vmem((6, 4, 128), F32),
             vmem((6, 4, 256, 128), I16),
@@ -499,6 +520,7 @@
             vmem((2, 2, 128, 512), I16),
             vmem((2, 2, 4, 128), F32),
             vmem((2, 8, 128), F32),
+            pltpu.SemaphoreType.DMA((2,)),
             pltpu.SemaphoreType.DMA((128,)),
             pltpu.SemaphoreType.DMA((128,)),
         ],

time: 90.4 us -> 85.3 us (0.944)
  Pallas kernels: 85.1 us -> 79.9 us
    pallas_call x1, Pallas kernels: 85.1 us -> 79.9 us  [local(): pl.pallas_call(kernel, out_shape=(jax.ShapeDtypeStruct((2, 128), F32), ja...]
where the time goes in v2:
time: 85.3 us; the launch traced here: 85.1 us
  Pallas kernels  79.9 us (94%)
  local copies, waits for them, and re-layouts  4.53 us (5%)
    pallas_call x1, Pallas kernels, local(): pl.pallas_call(kernel, out_shape=(jax.ShapeDtypeStruct((2, 128), F32), ja...  79.9 us
    unnamed x7, local copies, waits for them, and re-layouts  4.53 us

profile of v2, /device:TPU:1, one launch (start us, length us, event | category | flops | bytes accessed | tf_op | source)
XLA Modules:
  0.0 85.1 jit_solution(6455192150451951873)
XLA Ops:
  0.6 79.9 %shard_map.58 = (f32[2,128]{1,0:T(2,128)}, f32[256,1024]{1,0:T(8,128)}, f32[256,1024]{1,0:T(8,128)}) custom-call(bf16[256,1024]{1,0:T(8,128)(2,1)} %q_ref.1, bf16[256,1024]{1,0:T(8,128)(2,1)} %p_ref.1, s32[2,128]{1,0:T(2,128)} %bitcast.2), custom_call_target="tpu_custom_call" | custom-call | tf_op jit(solution)/shard_map/pallas_call | solution.py:482
  80.6 0.0 copy-start.1
  80.6 0.6 copy-done.1
  81.2 0.6 copy.9
  81.8 0.0 copy-start
  81.8 2.4 %copy.10 = f32[256,1024]{1,0:T(8,128)} copy(f32[256,1024]{1,0:T(8,128)} %get-tuple-element.13) | data formatting | bytes 2097152
  84.1 0.0 copy-done
  84.2 1.0 %copy.11 = f32[256,1024]{1,0:T(8,128)} copy(f32[256,1024]{1,0:T(8,128)S(1)} %copy-done) | data formatting | bytes 2097152
Async XLA Ops:
  80.6 0.6 copy-start.1
  81.8 2.4 %copy-start = (f32[256,1024]{1,0:T(8,128)S(1)}, f32[256,1024]{1,0:T(8,128)}, u32[]{:S(2)}) copy-start(f32[256,1024]{1,0:T(8,128)} %get-tuple-element.14) | copy-start | bytes 3145732

commit v3 on v2

--- a/solution.py
+++ b/solution.py
@@ -21,8 +21,8 @@
 
 
 def kernel(
-    q_ref, p_ref, pos_ref, loss_ref, gq_ref, gp_ref,
-    qb, pb, pt, sc, wb, wq, accq, accp, posb, st, stp, stx, stz, lser,
+    q_ref, p_ref, pos_ref, loss_ref, fin_ref, fins_ref, gp_ref,
+    qb, pb, pt, sc, wb, wq, accq, accp, posb, st, sm, stp, stx, stz, lser,
     sx, rq, ys, yss, yr, yrs, bs, bss, br, brs, az, azs, ar, ars, fin, fins, lossb, lsem, ssem, rsem,
 ):
     rows = lax.axis_index("rows")
@@ -67,9 +67,11 @@
     ]
     for fetch in fetches:
         fetch.start()
-    pl.semaphore_wait(barrier, len(peers))
+    pos_own = jnp.where(y_lo == 0, pos_ref[0:1, :], pos_ref[1:2, :])
+    posb[x, z] = jnp.broadcast_to(pos_own, (8, 128))
     for fetch in fetches:
         fetch.wait()
+    pl.semaphore_wait(barrier, len(peers))
 
     started, drained = [], set()
 
@@ -87,6 +89,7 @@
         drained.add(next(k for k, other in enumerate(started) if other is copy))
         copy.wait_send()
 
+    pos_x = [send(posb.at[x, z], posb.at[x, z], peer) for peer in x_peers]
     lo, hi = pl.ds(0, 128), pl.ds(128, 128)
     pu0 = send(pb.at[0, lo], pb.at[1, lo], y_up)
     pd0 = send(pb.at[0, hi], pb.at[2, hi], y_down)
@@ -107,9 +110,6 @@
     down2 = [send(own, part(me), b_down)]
     pu1 = send(pb.at[0, hi], pb.at[1, hi], y_up)
     pd1 = send(pb.at[0, lo], pb.at[2, lo], y_down)
-    pos_own = jnp.where(y_lo == 0, pos_ref[0:1, :], pos_ref[1:2, :])
-    posb[x, z] = jnp.broadcast_to(pos_own, (8, 128))
-    pos_x = [send(posb.at[x, z], posb.at[x, z], peer) for peer in x_peers]
 
     def turn(j):
         for k in range(4):
@@ -129,15 +129,15 @@
         up2.append(send(part(s), part(s), b_up))
         down2.append(send(part(s), part(s), b_down))
 
+    for copy in pos_x:
+        copy.wait_recv()
+    pos_z = [send(posb.at[:, z], posb.at[:, z], peer) for peer in z_peers]
     up1.wait_recv()
     fu1 = send(first(slot(a3, b)), first(slot(a3, b)), a_up)
     on(slot(a3, b))
     down1.wait_recv()
     fd1 = send(second(slot(a1, b)), second(slot(a1, b)), a_down)
     on(slot(a1, b))
-    for copy in pos_x:
-        copy.wait_recv()
-    pos_z = [send(posb.at[:, z], posb.at[:, z], peer) for peer in z_peers]
     fu1.wait_recv()
     fd1.wait_recv()
     on(slot(a2, b))
@@ -160,21 +160,17 @@
     pfu = send(pb.at[1, lo], pb.at[3, lo], y_up)
     pd0.wait_recv()
     pfd = send(pb.at[2, hi], pb.at[3, hi], y_down)
-    for copy in pos_z:
-        copy.wait_recv()
-
     def columns(s):
         return pl.ds(pl.multiple_of(s * 128, 128), 128)
 
+    def hits(s, j):
+        base = ((x * 4 + z) * 8 + y_of[j] * 2 + c) * 256
+        return lax.broadcasted_iota(jnp.int32, (256, 128), 0) == posb[s // 4, s % 4, 0:1, :] - base
+
     def mask(s, _):
-        where = posb[s // 4, s % 4, 0:1, :]
         for j in range(4):
-            base = ((x * 4 + z) * 8 + y_of[j] * 2 + c) * 256
-            hit = lax.broadcasted_iota(jnp.int32, (256, 128), 0) == where - base
-            wb[j * 256 : (j + 1) * 256, columns(s)] = jnp.where(hit, 1.0, 0.0).astype(BF16)
+            wb[j * 256 : (j + 1) * 256, columns(s)] = jnp.where(hits(s, j), 1.0, 0.0).astype(BF16)
         return 0
-
-    lax.fori_loop(0, 16, mask, 0)
 
     def product(begin, end, s1, s2):
         block = pb[begin // 256 : end // 256].reshape(end - begin, 1024)
@@ -185,8 +181,10 @@
     def statistics(begin, end, s1, s2):
         for s in (s1, s2):
             v = sc[s, begin:end]
-            hit = wb[begin:end, columns(s)].astype(F32)
-            chosen = jnp.sum(v * hit, axis=0, keepdims=True)
+            chosen = jnp.zeros((1, 128), F32)
+            for j in range(begin // 256, end // 256):
+                block = v[j * 256 - begin : (j + 1) * 256 - begin]
+                chosen += jnp.sum(jnp.where(hits(s, j), block, 0.0), axis=0, keepdims=True)
             best = jnp.max(v, axis=0, keepdims=True)
             row = pl.ds(s, 1)
             if begin == 0:
@@ -212,6 +210,9 @@
 
     along(1)
     along(2)
+    for copy in pos_z:
+        copy.wait_recv()
+    lax.fori_loop(0, 16, mask, 0)
     early = [
         (slot(a, b3), slot(a, b1)),
         (slot(a3, b), slot(a1, b)),
@@ -219,88 +220,111 @@
         (slot(a1, b3), slot(a1, b1)),
     ]
     late = [
-        (slot(a, b), slot(a2, b)),
-        (slot(a2, b3), slot(a2, b1)),
-        (slot(a, b2), slot(a3, b2)),
-        (slot(a1, b2), slot(a2, b2)),
+        (slot(a, b2), slot(a2, b)),
+        (slot(a3, b2), slot(a2, b3)),
+        (slot(a1, b2), slot(a2, b1)),
+        (slot(a, b), slot(a2, b2)),
     ]
+
+    def last(t):
+        fu2[t].wait_recv()
+        fd2[t].wait_recv()
+        over(slot(line[t], b2))
+
     landed(0, 1, 3, 4)
     score((0, 256, *early[0]), (0, 256, *early[1]))
     along(3)
     landed(5, 6, 7, 8)
     score((0, 256, *early[2]), (0, 256, *early[3]))
-    for t in range(4):
-        fu2[t].wait_recv()
-        fd2[t].wait_recv()
-        over(slot(line[t], b2))
     pu1.wait_recv()
     pd1.wait_recv()
     turn(1)
     turn(2)
-    score(*[(256, 768, *pair) for pair in early])
-    landed(2, 9, 10, 11, 12, 13, 14)
-    score(*[(0, 768, *pair) for pair in late])
+    score(*[(256, 768, *pair) for pair in early[:2]])
+    last(0)
+    last(1)
+    score(*[(256, 768, *pair) for pair in early[2:]])
+    last(2)
+    landed(2, 11)
+    score((0, 768, *late[0]))
+    last(3)
+    landed(9, 12)
+    score((0, 768, *late[1]))
+    landed(10, 13)
+    score((0, 768, *late[2]))
     pfu.wait_recv()
     pfd.wait_recv()
-    score(*[(768, 1024, 2 * g, 2 * g + 1) for g in range(8)])
-
-    stat = send(st, stp, partner)
-
-    def onehot_p(k, _):
+    score(*[(768, 1024, *pair) for pair in early + late[:3]])
+    landed(14)
+    score((0, 1024, *late[3]))
+
+    lser[0] = st[0]
+    sm[0], sm[1] = st[0] + jnp.log(st[1]), st[2]
+    stat = send(sm, stp, partner)
+
+    def meanwhile(k, _):
         col = pl.ds(pl.multiple_of(k * 256, 256), 256)
         qk = qb[:, :, col].reshape(2048, 256)
+        for t in range(4):
+            s = 4 * k + t
+            sc[s] = jnp.exp(sc[s] - lser[0, pl.ds(s, 1), :])
         d = jnp.dot(wb[...], qk, preferred_element_type=F32)
         for j in range(4):
             accp[j, :, col] = -d[j * 256 : (j + 1) * 256]
         return 0
 
     def join(others):
-        best = st[0]
+        best, chosen = sm[0], sm[1]
         for other in others:
             best = jnp.maximum(best, other[0])
-        total = st[1] * jnp.exp(st[0] - best)
-        chosen = st[2]
+            chosen = chosen + other[1]
+        total = jnp.exp(sm[0] - best)
         for other in others:
-            total = total + other[1] * jnp.exp(other[0] - best)
-            chosen = chosen + other[2]
-        return best, total, chosen
-
-    lax.fori_loop(0, 1, onehot_p, 0)
+            total = total + jnp.exp(other[0] - best)
+        return best + jnp.log(total), chosen
+
+    lax.fori_loop(0, 1, meanwhile, 0)
     turn(3)
     stat.wait_recv()
     drain(stat)
-    st[0], st[1], st[2] = join([stp])
-    copies = [send(st, stx.at[k], x_peers[k]) for k in range(3)]
-    lax.fori_loop(1, 3, onehot_p, 0)
+    sm[0], sm[1] = join([stp])
+    copies = [send(sm, stx.at[k], x_peers[k]) for k in range(3)]
+    lax.fori_loop(1, 3, meanwhile, 0)
     for copy in copies:
         copy.wait_recv()
         drain(copy)
-    st[0], st[1], st[2] = join([stx.at[k] for k in range(3)])
-    copies = [send(st, stz.at[k], z_peers[k]) for k in range(3)]
-    lax.fori_loop(3, 4, onehot_p, 0)
+    sm[0], sm[1] = join([stx.at[k] for k in range(3)])
+    copies = [send(sm, stz.at[k], z_peers[k]) for k in range(3)]
+    lax.fori_loop(3, 4, meanwhile, 0)
     for copy in copies:
         copy.wait_recv()
         drain(copy)
-    best, total, chosen = join([stz.at[k] for k in range(3)])
-    lse = best + jnp.log(total)
-    lser[0] = lse
+    lse, chosen = join([stz.at[k] for k in range(3)])
+    lser[0] = jnp.exp(lser[0] - lse)
     lser[1] = lse - chosen
     v = jnp.exp(chosen - lse) - 1.0
     exact = v.astype(BF16).astype(F32)
     plain = (v == 0.0) | (exact == 0.0)
-    lser[2] = jnp.where(plain, 1.0, exact / jnp.where(plain, 1.0, v))
+    lser[2] = jnp.where(plain, 1.0, exact / jnp.where(plain, 1.0, v)) * lser[0]
+    lser[4] = exact
     lser[3] = jnp.where(plain, 1.0, v / jnp.where(plain, 1.0, exact))
     lossb[y_lo] = jnp.broadcast_to(lser[1, pl.ds(x * 4 + z, 1), :], (8, 128))
     loss_copy = send(lossb.at[y_lo], lossb.at[y_lo], y_pair)
 
+    a_order, b_order = [a2, a3, a1, a], [b2, b3, b1, b]
+
     def weigh(s, _):
-        w = jnp.exp(sc[s] - lser[0, pl.ds(s, 1), :])
-        less = (w - wb[:, columns(s)].astype(F32)) * lser[2, pl.ds(s, 1), :]
-        wb[:, columns(s)] = w.astype(BF16)
-        wq[:, columns(s)] = less.astype(BF16)
+        row = pl.ds(s, 1)
+        for j in range(4):
+            part = pl.ds(j * 256, 256)
+            e = sc[s, part]
+            wb[part, columns(s)] = (e * lser[0, row, :]).astype(BF16)
+            less = jnp.where(hits(s, j), lser[4, row, :], e * lser[2, row, :])
+            wq[part, columns(s)] = less.astype(BF16)
         return 0
 
-    lax.fori_loop(0, 16, weigh, 0)
+    def weights_of(slots):
+        return jnp.concatenate([wq[:, columns(s)] for s in slots], axis=1)
 
     def grad_p(h):
         def step(k, _):
@@ -316,25 +340,19 @@
     mine_d = pl.ds(pl.multiple_of(c * 512, 512), 512)
     other_d = pl.ds(pl.multiple_of((1 - c) * 512, 512), 512)
     halves = (pl.ds(0, 256), pl.ds(256, 256))
-    a_order, b_order = [a2, a3, a1, a], [b2, b3, b1, b]
-
     def mine_slots(k):
         return [slot(da, b_order[k]) for da in a_order]
 
-    def other_slots(k):
-        return [slot(a_order[k], db) for db in b_order]
-
-    def weights_of(slots):
-        return jnp.concatenate([wq[:, columns(s)] for s in slots], axis=1)
-
     swaps = []
 
-    def grad_q(k):
-        slots = other_slots(k)
+    def grad_other(k):
+        slots = [slot(a_order[k], db) for db in b_order]
         d = jnp.dot(pt[other_d, :], weights_of(slots), preferred_element_type=F32)
         for t in range(4):
             sx[k, t] = d[:, t * 128 : (t + 1) * 128]
         swaps.append(send(sx.at[k], rq.at[k], partner))
+
+    def grad_mine(k):
         slots = mine_slots(k)
         d = jnp.dot(pt[mine_d, :], weights_of(slots), preferred_element_type=F32)
         for t, s in enumerate(slots):
@@ -375,8 +393,8 @@
 
     def end_p(h):
         part = pl.ds(h * 512, 512)
-        gp_ref[lo, part] = accp[0, lo, part] + arrive_p(h, 3, hops_p[h, 3]) + arrive_p(h, 4, hops_p[h, 4])
-        gp_ref[hi, part] = accp[0, hi, part] + arrive_p(h, 2, hops_p[h, 2]) + arrive_p(h, 5, hops_p[h, 5])
+        accp[0, lo, part] += arrive_p(h, 3, hops_p[h, 3]) + arrive_p(h, 4, hops_p[h, 4])
+        accp[0, hi, part] += arrive_p(h, 2, hops_p[h, 2]) + arrive_p(h, 5, hops_p[h, 5])
 
     def hop_b(n, k, side, device):
         for t, s in enumerate(mine_slots(k)):
@@ -400,26 +418,31 @@
             copy.wait_recv()
         accq[slot(da, b), halves[side]] += restored(ar[n], ars[n, 0:1, :])
 
-    grad_q(0)
-    grad_q(1)
+    lax.fori_loop(0, 16, weigh, 0)
+    grad_other(0)
+    grad_mine(0)
+    grad_p(0)
+    begin_p(0)
     swapped(0)
     qu_a = hop_b(0, 0, 0, b_up)
     qd_a = hop_b(1, 0, 1, b_down)
-    grad_q(2)
+    grad_other(1)
+    grad_other(2)
+    grad_mine(1)
+    grad_mine(2)
     swapped(1)
     qd_b = hop_b(2, 1, 0, b_down)
-    grad_p(0)
-    begin_p(0)
     swapped(2)
     qu_b = hop_b(3, 2, 1, b_up)
-    grad_q(3)
+    grad_other(3)
+    grad_mine(3)
     arrive_b(0, qu_a, 2, 0)
     qu_c = hop_b(4, 2, 0, b_up)
     arrive_b(1, qd_a, 1, 1)
     qd_c = hop_b(5, 1, 1, b_down)
+    relay_p(0)
     grad_p(1)
     begin_p(1)
-    relay_p(0)
     swapped(3)
     arrive_b(2, qd_b, 3, 0)
     arrive_b(3, qu_b, 3, 1)
@@ -448,46 +471,62 @@
 
     out1 = share(y_lo, y_pair)
     out2 = share(y_lo, partner)
+
+    def leave(h, core, sem):
+        copy = pltpu.make_async_copy(fin.at[h, core], fin_ref.at[h, core], lsem.at[sem])
+        copy.start()
+        left.append(copy)
+
+    left = []
+    leave(y_lo, c, 0)
     end_p(0)
     end_p(1)
+    copy = pltpu.make_async_copy(accp.at[0], gp_ref, lsem.at[1])
+    copy.start()
+    left.append(copy)
     loss_copy.wait_recv()
     loss_ref[0:1, :] = lossb[0, 0:1, :]
     loss_ref[1:2, :] = lossb[1, 0:1, :]
     for copy in out1:
         copy.wait_recv()
     out3 = share(1 - y_lo, partner)
-
-    def finish(h, core):
-        scale = jnp.concatenate([fins[h, core, k : k + 1, :] for k in range(4)], axis=1)
-        gq_ref[pl.ds(pl.multiple_of(h * 128, 128), 128), pl.ds(pl.multiple_of(core * 512, 512), 512)] = (
-            restored(fin[h, core], scale)
-        )
-
-    finish(y_lo, c)
-    finish(1 - y_lo, c)
+    leave(1 - y_lo, c, 2)
     for copy in out2:
         copy.wait_recv()
-    finish(y_lo, 1 - c)
+    leave(y_lo, 1 - c, 3)
     for copy in out3:
         copy.wait_recv()
-    finish(1 - y_lo, 1 - c)
+    leave(1 - y_lo, 1 - c, 4)
+    fins_ref[...] = fins[...]
+    for copy in left:
+        copy.wait()
     for k, copy in enumerate(started):
         if k not in drained:
             copy.wait_send()
 
 
+def finish(fin_ref, fins_ref, gp_ref, loss_ref, gq_out, gp_out, loss_out):
+    for core in range(2):
+        scale = jnp.concatenate([fins_ref[0, core, k : k + 1, :] for k in range(4)], axis=1)
+        gq_out[:, core * 512 : (core + 1) * 512] = restored(fin_ref[0, core], scale)
+    gp_out[...] = gp_ref[...]
+    loss_out[...] = loss_ref[...]
+
+
 def local(queries, passages, positive):
     vmem = pltpu.VMEM
     space = pl.BlockSpec(memory_space=vmem)
-    loss, gq, gp = pl.pallas_call(
+    anywhere = pl.BlockSpec(memory_space=pl.ANY)
+    loss, fin, fins, gp = pl.pallas_call(
         kernel,
         out_shape=(
             jax.ShapeDtypeStruct((2, 128), F32),
-            jax.ShapeDtypeStruct((256, 1024), F32),
+            jax.ShapeDtypeStruct((2, 2, 128, 512), I16),
+            jax.ShapeDtypeStruct((2, 2, 4, 128), F32),
             jax.ShapeDtypeStruct((256, 1024), F32),
         ),
-        in_specs=[pl.BlockSpec(memory_space=pl.ANY)] * 2 + [space],
-        out_specs=(space,) * 3,
+        in_specs=[anywhere, anywhere, space],
+        out_specs=(space, anywhere, space, anywhere),
         scratch_shapes=[
             vmem((16, 128, 1024), BF16),
             vmem((4, 256, 1024), BF16),
@@ -499,10 +538,11 @@
             vmem((4, 256, 1024), F32),
             vmem((4, 4, 8, 128), jnp.int32),
             vmem((3, 16, 128), F32),
-            vmem((3, 16, 128), F32),
-            vmem((3, 3, 16, 128), F32),
-            vmem((3, 3, 16, 128), F32),
-            vmem((4, 16, 128), F32),
+            vmem((2, 16, 128), F32),
+            vmem((2, 16, 128), F32),
+            vmem((3, 2, 16, 128), F32),
+            vmem((3, 2, 16, 128), F32),
+            vmem((5, 16, 128), F32),
             vmem((4, 4, 512, 128), F32),
             vmem((4, 4, 512, 128), F32),
             vmem((2, 6, 128, 512), I16),
@@ -520,7 +560,7 @@
             vmem((2, 2, 128, 512), I16),
             vmem((2, 2, 4, 128), F32),
             vmem((2, 8, 128), F32),
-            pltpu.SemaphoreType.DMA((2,)),
+            pltpu.SemaphoreType.DMA((5,)),
             pltpu.SemaphoreType.DMA((128,)),
             pltpu.SemaphoreType.DMA((128,)),
         ],
@@ -528,6 +568,26 @@
             collective_id=0, has_side_effects=True, vmem_limit_bytes=66_000_000
         ),
     )(queries, passages, positive.reshape(2, 128))
+    gq, gp, loss = pl.pallas_call(
+        finish,
+        grid=(2,),
+        out_shape=(
+            jax.ShapeDtypeStruct((256, 1024), F32),
+            jax.ShapeDtypeStruct((256, 1024), F32),
+            jax.ShapeDtypeStruct((2, 128), F32),
+        ),
+        in_specs=[
+            pl.BlockSpec((1, 2, 128, 512), lambda h: (h, 0, 0, 0)),
+            pl.BlockSpec((1, 2, 4, 128), lambda h: (h, 0, 0, 0)),
+            pl.BlockSpec((128, 1024), lambda h: (h, 0)),
+            pl.BlockSpec((2, 128), lambda h: (0, 0)),
+        ],
+        out_specs=(
+            pl.BlockSpec((128, 1024), lambda h: (h, 0)),
+            pl.BlockSpec((128, 1024), lambda h: (h, 0)),
+            pl.BlockSpec((2, 128), lambda h: (0, 0)),
+        ),
+    )(fin, fins, gp, loss)
     return loss.reshape(256), gq, gp
 
 

time: 85.3 us -> 81.6 us (0.957)
  local copies, waits for them, and re-layouts: 4.53 us -> 0 us
  Pallas kernels: 79.9 us -> 80.8 us
    unnamed x7 -> x0, local copies, waits for them, and re-layouts: 4.53 us -> none
    pallas_call x0 -> x1, Pallas kernels: none -> 2.53 us  [local(): pl.pallas_call(finish, grid=(2,), out_shape=(jax.ShapeDtypeStruct((256, 1...]
    pallas_call x1, Pallas kernels: 79.9 us -> 78.3 us  [local(): pl.pallas_call(kernel, out_shape=(jax.ShapeDtypeStruct((2, 128), F32), ja...]
where the time goes in v3:
time: 81.6 us; the launch traced here: 81.4 us
  Pallas kernels  80.8 us (99%)
    pallas_call x1, Pallas kernels, local(): pl.pallas_call(kernel, out_shape=(jax.ShapeDtypeStruct((2, 128), F32), ja...  78.3 us
    pallas_call x1, Pallas kernels, local(): pl.pallas_call(finish, grid=(2,), out_shape=(jax.ShapeDtypeStruct((256, 1...  2.53 us

profile of v3, /device:TPU:1, one launch (start us, length us, event | category | flops | bytes accessed | tf_op | source)
XLA Modules:
  0.0 81.4 jit_solution(581416109403686345)
XLA Ops:
  0.6 78.3 %shard_map.58 = (f32[2,128]{1,0:T(2,128)}, s16[2,2,128,512]{3,2,1,0:T(8,128)(2,1)}, f32[2,2,4,128]{3,2,1,0:T(4,128)}, f32[256,1024]{1,0:T(8,128)}) custom-call(bf16[256,1024]{1,0:T(8,128)(2,1)} %q_ref.1, bf16[256,1024]{1,0:T(8,128)(2,1)} %p_ref.1, s32[2,128]{1,0:T(2,128)} %bitcast.2), custom_call_target="tpu_custom_call" | custom-call | tf_op jit(solution)/shard_map/pallas_call | solution.py:520
  78.9 2.5 %shard_map.59 = (f32[256,1024]{1,0:T(8,128)}, f32[256,1024]{1,0:T(8,128)}, f32[2,128]{1,0:T(2,128)}) custom-call(s16[2,2,128,512]{3,2,1,0:T(8,128)(2,1)} %get-tuple-element.10.fin_ref, f32[2,2,4,128]{3,2,1,0:T(4,128)} %get-tuple-element.11.fins_ref, f32[256,1024]{1,0:T(8,128)} %get-tuple-element.12.gp_ref, f32[2,128]{1,0:T(2,128)} %get-tuple-element.13.loss_ref), custom_call_target="tpu_custom_call" | custom-call | tf_op jit(solution)/shard_map/pallas_call | solution.py:571

commit v4 on v3

--- a/solution.py
+++ b/solution.py
@@ -9,6 +9,7 @@
 F32 = jnp.float32
 BF16 = jnp.bfloat16
 I16 = jnp.int16
+SENDS, RECEIVES = 32, 137
 
 
 def quantized(v):
@@ -22,7 +23,7 @@
 
 def kernel(
     q_ref, p_ref, pos_ref, loss_ref, fin_ref, fins_ref, gp_ref,
-    qb, pb, pt, sc, wb, wq, accq, accp, posb, st, sm, stp, stx, stz, lser,
+    qb, qt, pb, pt, sc, ob, wb, wq, accq, accp, posb, st, sm, stp, stx, stz, lser,
     sx, rq, ys, yss, yr, yrs, bs, bss, br, brs, az, azs, ar, ars, fin, fins, lossb, lsem, ssem, rsem,
 ):
     rows = lax.axis_index("rows")
@@ -77,8 +78,11 @@
 
     def send(src, dst, device):
         index = len(started)
+        if index >= SENDS and index - SENDS not in drained:
+            drained.add(index - SENDS)
+            started[index - SENDS].wait_send()
         copy = pltpu.make_async_remote_copy(
-            src_ref=src, dst_ref=dst, send_sem=ssem.at[index], recv_sem=rsem.at[index],
+            src_ref=src, dst_ref=dst, send_sem=ssem.at[index % SENDS], recv_sem=rsem.at[index],
             device_id=device, device_id_type=MESH,
         )
         copy.start()
@@ -168,41 +172,49 @@
         return lax.broadcasted_iota(jnp.int32, (256, 128), 0) == posb[s // 4, s % 4, 0:1, :] - base
 
     def mask(s, _):
-        for j in range(4):
+        ob[:, columns(s)] = jnp.where(hits(s, 0), 1.0, 0.0).astype(BF16)
+        for j in range(1, 4):
             wb[j * 256 : (j + 1) * 256, columns(s)] = jnp.where(hits(s, j), 1.0, 0.0).astype(BF16)
         return 0
 
+    def flip(*slots):
+        for s in slots:
+            for k in range(4):
+                qt[k * 256 : (k + 1) * 256, columns(s)] = qb[s, :, k * 256 : (k + 1) * 256].T
+
     def product(begin, end, s1, s2):
-        block = pb[begin // 256 : end // 256].reshape(end - begin, 1024)
-        both = jnp.concatenate([qb[s1], qb[s2]], axis=0)
-        d = lax.dot_general(block, both, (((1,), (1,)), ((), ())), preferred_element_type=F32)
-        sc[s1, begin:end], sc[s2, begin:end] = d[:, :128], d[:, 128:]
+        both = jnp.concatenate([qt[:, columns(s1)], qt[:, columns(s2)]], axis=1)
+        for j in range(begin // 256, end // 256):
+            part = pl.ds(j * 256, 256)
+            d = jnp.dot(pb[j], both, preferred_element_type=F32)
+            sc[s1, part], sc[s2, part] = d[:, :128], d[:, 128:]
 
     def statistics(begin, end, s1, s2):
         for s in (s1, s2):
-            v = sc[s, begin:end]
-            chosen = jnp.zeros((1, 128), F32)
+            v = sc[s, begin:end].reshape((end - begin) // 8, 8, 128)
+            chosen = jnp.zeros((8, 128), F32)
             for j in range(begin // 256, end // 256):
-                block = v[j * 256 - begin : (j + 1) * 256 - begin]
-                chosen += jnp.sum(jnp.where(hits(s, j), block, 0.0), axis=0, keepdims=True)
-            best = jnp.max(v, axis=0, keepdims=True)
-            row = pl.ds(s, 1)
+                block = jnp.where(hits(s, j), sc[s, j * 256 : (j + 1) * 256], 0.0)
+                chosen += jnp.sum(block.reshape(32, 8, 128), axis=0)
+            best = jnp.max(v, axis=0)
             if begin == 0:
-                total = jnp.sum(jnp.exp(v - best), axis=0, keepdims=True)
+                total = jnp.sum(jnp.exp(v - best), axis=0)
             else:
-                old = st[0, row, :]
+                old = st[0, s]
                 best = jnp.maximum(best, old)
-                total = jnp.sum(jnp.exp(v - best), axis=0, keepdims=True)
-                total = total + st[1, row, :] * jnp.exp(old - best)
-                chosen = chosen + st[2, row, :]
-            st[0, row, :], st[1, row, :], st[2, row, :] = best, total, chosen
+                total = jnp.sum(jnp.exp(v - best), axis=0)
+                total = total + st[1, s] * jnp.exp(old - best)
+                chosen = chosen + st[2, s]
+            st[0, s], st[1, s], st[2, s] = best, total, chosen
+
+    pending = []
 
     def score(*items):
-        for k, item in enumerate(items):
-            if k:
-                statistics(*items[k - 1])
+        for item in items:
+            if pending:
+                statistics(*pending.pop())
             product(*item)
-        statistics(*items[-1])
+            pending.append(item)
 
     def landed(*indices):
         for k in indices:
@@ -231,10 +243,13 @@
         fd2[t].wait_recv()
         over(slot(line[t], b2))
 
+    flip(me)
     landed(0, 1, 3, 4)
+    flip(*early[0], *early[1])
     score((0, 256, *early[0]), (0, 256, *early[1]))
     along(3)
     landed(5, 6, 7, 8)
+    flip(*early[2], *early[3])
     score((0, 256, *early[2]), (0, 256, *early[3]))
     pu1.wait_recv()
     pd1.wait_recv()
@@ -246,20 +261,27 @@
     score(*[(256, 768, *pair) for pair in early[2:]])
     last(2)
     landed(2, 11)
+    flip(*late[0])
     score((0, 768, *late[0]))
     last(3)
     landed(9, 12)
+    flip(*late[1])
     score((0, 768, *late[1]))
     landed(10, 13)
+    flip(*late[2])
     score((0, 768, *late[2]))
     pfu.wait_recv()
     pfd.wait_recv()
     score(*[(768, 1024, *pair) for pair in early + late[:3]])
     landed(14)
+    flip(late[3][1])
     score((0, 1024, *late[3]))
-
-    lser[0] = st[0]
-    sm[0], sm[1] = st[0] + jnp.log(st[1]), st[2]
+    statistics(*pending.pop())
+
+    most = jnp.max(st[0], axis=1)
+    total = jnp.sum(st[1] * jnp.exp(st[0] - most[:, None, :]), axis=1)
+    lser[0] = most
+    sm[0], sm[1] = most + jnp.log(total), jnp.sum(st[2], axis=1)
     stat = send(sm, stp, partner)
 
     def meanwhile(k, _):
@@ -268,9 +290,9 @@
         for t in range(4):
             s = 4 * k + t
             sc[s] = jnp.exp(sc[s] - lser[0, pl.ds(s, 1), :])
-        d = jnp.dot(wb[...], qk, preferred_element_type=F32)
-        for j in range(4):
-            accp[j, :, col] = -d[j * 256 : (j + 1) * 256]
+        for j in range(1, 4):
+            d = jnp.dot(wb[j * 256 : (j + 1) * 256], qk, preferred_element_type=F32)
+            accp[j, :, col] = -d
         return 0
 
     def join(others):
@@ -327,36 +349,48 @@
         return jnp.concatenate([wq[:, columns(s)] for s in slots], axis=1)
 
     def grad_p(h):
-        def step(k, _):
-            col = pl.ds(pl.multiple_of(k * 256, 256), 256)
-            qk = qb[:, :, col].reshape(2048, 256)
-            d = jnp.dot(wb[...], qk, preferred_element_type=F32)
-            for j in range(4):
-                accp[j, :, col] += d[j * 256 : (j + 1) * 256]
-            return 0
-
-        lax.fori_loop(2 * h, 2 * h + 2, step, 0)
-
-    mine_d = pl.ds(pl.multiple_of(c * 512, 512), 512)
-    other_d = pl.ds(pl.multiple_of((1 - c) * 512, 512), 512)
+        col = pl.ds(h * 256, 256)
+        qk = qb[:, :, col].reshape(2048, 256)
+        for j in (3, 2, 1):
+            accp[j, :, col] += jnp.dot(
+                wb[j * 256 : (j + 1) * 256], qk, preferred_element_type=F32
+            )
+
+    def grad_own(h):
+        col = pl.ds(h * 256, 256)
+        qk = qb[:, :, col].reshape(2048, 256)
+        d = jnp.dot(wb[0:256], qk, preferred_element_type=F32)
+        accp[0, :, col] = d - jnp.dot(ob[...], qk, preferred_element_type=F32)
+
     halves = (pl.ds(0, 256), pl.ds(256, 256))
     def mine_slots(k):
         return [slot(da, b_order[k]) for da in a_order]
 
     swaps = []
 
+    def grad_half(d_rows, slots, store):
+        for n in (0, 2):
+            right = weights_of(slots[n : n + 2])
+            for m in range(2):
+                left = pt[pl.ds(pl.multiple_of(d_rows * 512 + m * 256, 256), 256), :]
+                d = jnp.dot(left, right, preferred_element_type=F32)
+                for t in range(2):
+                    store(n + t, pl.ds(m * 256, 256), d[:, t * 128 : (t + 1) * 128])
+
     def grad_other(k):
-        slots = [slot(a_order[k], db) for db in b_order]
-        d = jnp.dot(pt[other_d, :], weights_of(slots), preferred_element_type=F32)
-        for t in range(4):
-            sx[k, t] = d[:, t * 128 : (t + 1) * 128]
+        def store(t, part, d):
+            sx[k, t, part] = d
+
+        grad_half(1 - c, [slot(a_order[k], db) for db in b_order], store)
         swaps.append(send(sx.at[k], rq.at[k], partner))
 
     def grad_mine(k):
         slots = mine_slots(k)
-        d = jnp.dot(pt[mine_d, :], weights_of(slots), preferred_element_type=F32)
-        for t, s in enumerate(slots):
-            accq[s] = d[:, t * 128 : (t + 1) * 128]
+
+        def store(t, part, d):
+            accq[slots[t], part] = d
+
+        grad_half(c, slots, store)
 
     def swapped(k):
         swaps[k].wait_recv()
@@ -364,16 +398,16 @@
             accq[s] += rq[k, t]
 
     def hop_p(h, n, j, half, device):
-        v, scale = quantized(accp[j, half, h * 512 : (h + 1) * 512])
+        v, scale = quantized(accp[j, half, h * 256 : (h + 1) * 256])
         ys[h, n] = v
-        for k in range(4):
+        for k in range(2):
             yss[h, n, k : k + 1, :] = scale[:, k * 128 : (k + 1) * 128]
         return send(ys.at[h, n], yr.at[h, n], device), send(yss.at[h, n], yrs.at[h, n], device)
 
     def arrive_p(h, n, hop):
         for copy in hop:
             copy.wait_recv()
-        scale = jnp.concatenate([yrs[h, n, k : k + 1, :] for k in range(4)], axis=1)
+        scale = jnp.concatenate([yrs[h, n, k : k + 1, :] for k in range(2)], axis=1)
         return restored(yr[h, n], scale)
 
     hops_p = {}
@@ -385,14 +419,14 @@
         hops_p[h, 3] = hop_p(h, 3, 1, lo, y_down)
 
     def relay_p(h):
-        part = pl.ds(h * 512, 512)
+        part = pl.ds(h * 256, 256)
         accp[2, lo, part] += arrive_p(h, 0, hops_p[h, 0])
         hops_p[h, 4] = hop_p(h, 4, 2, lo, y_up)
         accp[1, hi, part] += arrive_p(h, 1, hops_p[h, 1])
         hops_p[h, 5] = hop_p(h, 5, 1, hi, y_down)
 
     def end_p(h):
-        part = pl.ds(h * 512, 512)
+        part = pl.ds(h * 256, 256)
         accp[0, lo, part] += arrive_p(h, 3, hops_p[h, 3]) + arrive_p(h, 4, hops_p[h, 4])
         accp[0, hi, part] += arrive_p(h, 2, hops_p[h, 2]) + arrive_p(h, 5, hops_p[h, 5])
 
@@ -420,43 +454,52 @@
 
     lax.fori_loop(0, 16, weigh, 0)
     grad_other(0)
+    grad_other(1)
     grad_mine(0)
     grad_p(0)
     begin_p(0)
     swapped(0)
     qu_a = hop_b(0, 0, 0, b_up)
     qd_a = hop_b(1, 0, 1, b_down)
-    grad_other(1)
     grad_other(2)
     grad_mine(1)
-    grad_mine(2)
     swapped(1)
     qd_b = hop_b(2, 1, 0, b_down)
+    grad_mine(2)
+    grad_p(1)
+    begin_p(1)
     swapped(2)
     qu_b = hop_b(3, 2, 1, b_up)
-    grad_other(3)
-    grad_mine(3)
+    grad_p(2)
+    begin_p(2)
+    relay_p(0)
     arrive_b(0, qu_a, 2, 0)
     qu_c = hop_b(4, 2, 0, b_up)
     arrive_b(1, qd_a, 1, 1)
     qd_c = hop_b(5, 1, 1, b_down)
-    relay_p(0)
-    grad_p(1)
-    begin_p(1)
+    grad_p(3)
+    begin_p(3)
+    relay_p(1)
+    grad_other(3)
+    grad_mine(3)
+    grad_own(0)
+    relay_p(2)
     swapped(3)
     arrive_b(2, qd_b, 3, 0)
     arrive_b(3, qu_b, 3, 1)
+    arrive_b(5, qd_c, 3, 1)
     arrive_b(4, qu_c, 3, 0)
-    arrive_b(5, qd_c, 3, 1)
     vu_a = hop_a(0, a2, 0, a_up)
     vd_a = hop_a(1, a2, 1, a_down)
     vd_b = hop_a(2, a3, 0, a_down)
     vu_b = hop_a(3, a1, 1, a_up)
-    relay_p(1)
+    relay_p(3)
+    grad_own(1)
     arrive_a(0, vu_a, a1, 0)
     vu_c = hop_a(4, a1, 0, a_up)
     arrive_a(1, vd_a, a3, 1)
     vd_c = hop_a(5, a3, 1, a_down)
+    grad_own(2)
     arrive_a(2, vd_b, a, 0)
     arrive_a(3, vu_b, a, 1)
     arrive_a(4, vu_c, a, 0)
@@ -479,8 +522,9 @@
 
     left = []
     leave(y_lo, c, 0)
-    end_p(0)
-    end_p(1)
+    grad_own(3)
+    for h in range(4):
+        end_p(h)
     copy = pltpu.make_async_copy(accp.at[0], gp_ref, lsem.at[1])
     copy.start()
     left.append(copy)
@@ -529,15 +573,17 @@
         out_specs=(space, anywhere, space, anywhere),
         scratch_shapes=[
             vmem((16, 128, 1024), BF16),
+            vmem((1024, 2048), BF16),
             vmem((4, 256, 1024), BF16),
             vmem((1024, 1024), BF16),
             vmem((16, 1024, 128), F32),
+            vmem((256, 2048), BF16),
             vmem((1024, 2048), BF16),
             vmem((1024, 2048), BF16),
             vmem((16, 512, 128), F32),
             vmem((4, 256, 1024), F32),
             vmem((4, 4, 8, 128), jnp.int32),
-            vmem((3, 16, 128), F32),
+            vmem((3, 16, 8, 128), F32),
             vmem((2, 16, 128), F32),
             vmem((2, 16, 128), F32),
             vmem((3, 2, 16, 128), F32),
@@ -545,10 +591,10 @@
             vmem((5, 16, 128), F32),
             vmem((4, 4, 512, 128), F32),
             vmem((4, 4, 512, 128), F32),
-            vmem((2, 6, 128, 512), I16),
-            vmem((2, 6, 4, 128), F32),
-            vmem((2, 6, 128, 512), I16),
-            vmem((2, 6, 4, 128), F32),
+            vmem((4, 6, 128, 256), I16),
+            vmem((4, 6, 2, 128), F32),
+            vmem((4, 6, 128, 256), I16),
+            vmem((4, 6, 2, 128), F32),
             vmem((6, 4, 256, 128), I16),
             vmem((6, 4, 128), F32),
             vmem((6, 4, 256, 128), I16),
@@ -561,8 +607,8 @@
             vmem((2, 2, 4, 128), F32),
             vmem((2, 8, 128), F32),
             pltpu.SemaphoreType.DMA((5,)),
-            pltpu.SemaphoreType.DMA((128,)),
-            pltpu.SemaphoreType.DMA((128,)),
+            pltpu.SemaphoreType.DMA((SENDS,)),
+            pltpu.SemaphoreType.DMA((RECEIVES,)),
         ],
         compiler_params=pltpu.CompilerParams(
             collective_id=0, has_side_effects=True, vmem_limit_bytes=66_000_000

time: 81.6 us -> 78.6 us (0.963)
  Pallas kernels: 80.8 us -> 77.8 us
    pallas_call x1, Pallas kernels: 78.3 us -> 75.3 us  [local(): pl.pallas_call(kernel, out_shape=(jax.ShapeDtypeStruct((2, 128), F32), ja...]
where the time goes in v4:
time: 78.6 us; the launch traced here: 78.4 us
  Pallas kernels  77.8 us (99%)
    pallas_call x1, Pallas kernels, local(): pl.pallas_call(kernel, out_shape=(jax.ShapeDtypeStruct((2, 128), F32), ja...  75.3 us
    pallas_call x1, Pallas kernels, local(): pl.pallas_call(finish, grid=(2,), out_shape=(jax.ShapeDtypeStruct((256, 1...  2.53 us

profile of v4, /device:TPU:1, one launch (start us, length us, event | category | flops | bytes accessed | tf_op | source)
XLA Modules:
  0.0 78.4 jit_solution(9643748754072791303)
XLA Ops:
  0.6 75.3 %shard_map.58 = (f32[2,128]{1,0:T(2,128)}, s16[2,2,128,512]{3,2,1,0:T(8,128)(2,1)}, f32[2,2,4,128]{3,2,1,0:T(4,128)}, f32[256,1024]{1,0:T(8,128)}) custom-call(bf16[256,1024]{1,0:T(8,128)(2,1)} %q_ref.1, bf16[256,1024]{1,0:T(8,128)(2,1)} %p_ref.1, s32[2,128]{1,0:T(2,128)} %bitcast.2), custom_call_target="tpu_custom_call" | custom-call | tf_op jit(solution)/shard_map/pallas_call | solution.py:564
  75.9 2.5 %shard_map.59 = (f32[256,1024]{1,0:T(8,128)}, f32[256,1024]{1,0:T(8,128)}, f32[2,128]{1,0:T(2,128)}) custom-call(s16[2,2,128,512]{3,2,1,0:T(8,128)(2,1)} %get-tuple-element.10.fin_ref, f32[2,2,4,128]{3,2,1,0:T(4,128)} %get-tuple-element.11.fins_ref, f32[256,1024]{1,0:T(8,128)} %get-tuple-element.12.gp_ref, f32[2,128]{1,0:T(2,128)} %get-tuple-element.13.loss_ref), custom_call_target="tpu_custom_call" | custom-call | tf_op jit(solution)/shard_map/pallas_call | solution.py:617

commit v5 on v4

--- a/solution.py
+++ b/solution.py
@@ -23,7 +23,7 @@
 
 def kernel(
     q_ref, p_ref, pos_ref, loss_ref, fin_ref, fins_ref, gp_ref,
-    qb, qt, pb, pt, sc, ob, wb, wq, accq, accp, posb, st, sm, stp, stx, stz, lser,
+    qb, qt, pb, pt, sc, ob, wb, wq, accq, accp, posi, posb, st, sm, stp, stx, stz, lser,
     sx, rq, ys, yss, yr, yrs, bs, bss, br, brs, az, azs, ar, ars, fin, fins, lossb, lsem, ssem, rsem,
 ):
     rows = lax.axis_index("rows")
@@ -65,13 +65,14 @@
     fetches = [
         pltpu.make_async_copy(p_ref, pb.at[0], lsem.at[0]),
         pltpu.make_async_copy(q_ref.at[pl.ds(y_lo * 128, 128)], qb.at[me], lsem.at[1]),
+        pltpu.make_async_copy(pos_ref, posi, lsem.at[2]),
     ]
     for fetch in fetches:
         fetch.start()
-    pos_own = jnp.where(y_lo == 0, pos_ref[0:1, :], pos_ref[1:2, :])
-    posb[x, z] = jnp.broadcast_to(pos_own, (8, 128))
     for fetch in fetches:
         fetch.wait()
+    pos_own = jnp.where(y_lo == 0, posi[0:1, :], posi[1:2, :])
+    posb[x, z] = jnp.broadcast_to(pos_own, (8, 128))
     pl.semaphore_wait(barrier, len(peers))
 
     started, drained = [], set()
@@ -142,6 +143,22 @@
     down1.wait_recv()
     fd1 = send(second(slot(a1, b)), second(slot(a1, b)), a_down)
     on(slot(a1, b))
+    def columns(s):
+        return pl.ds(pl.multiple_of(s * 128, 128), 128)
+
+    def hits(s, j):
+        base = ((x * 4 + z) * 8 + y_of[j] * 2 + c) * 256
+        return lax.broadcasted_iota(jnp.int32, (256, 128), 0) == posb[s // 4, s % 4, 0:1, :] - base
+
+    def mask(s, _):
+        ob[:, columns(s)] = jnp.where(hits(s, 0), 1.0, 0.0).astype(BF16)
+        for j in range(1, 4):
+            wb[j * 256 : (j + 1) * 256, columns(s)] = jnp.where(hits(s, j), 1.0, 0.0).astype(BF16)
+        return 0
+
+    for copy in pos_z:
+        copy.wait_recv()
+    lax.fori_loop(0, 16, mask, 0)
     fu1.wait_recv()
     fd1.wait_recv()
     on(slot(a2, b))
@@ -164,33 +181,20 @@
     pfu = send(pb.at[1, lo], pb.at[3, lo], y_up)
     pd0.wait_recv()
     pfd = send(pb.at[2, hi], pb.at[3, hi], y_down)
-    def columns(s):
-        return pl.ds(pl.multiple_of(s * 128, 128), 128)
-
-    def hits(s, j):
-        base = ((x * 4 + z) * 8 + y_of[j] * 2 + c) * 256
-        return lax.broadcasted_iota(jnp.int32, (256, 128), 0) == posb[s // 4, s % 4, 0:1, :] - base
-
-    def mask(s, _):
-        ob[:, columns(s)] = jnp.where(hits(s, 0), 1.0, 0.0).astype(BF16)
-        for j in range(1, 4):
-            wb[j * 256 : (j + 1) * 256, columns(s)] = jnp.where(hits(s, j), 1.0, 0.0).astype(BF16)
-        return 0
-
     def flip(*slots):
         for s in slots:
             for k in range(4):
                 qt[k * 256 : (k + 1) * 256, columns(s)] = qb[s, :, k * 256 : (k + 1) * 256].T
 
-    def product(begin, end, s1, s2):
-        both = jnp.concatenate([qt[:, columns(s1)], qt[:, columns(s2)]], axis=1)
+    def product(begin, end, *slots):
+        right = jnp.concatenate([qt[:, columns(s)] for s in slots], axis=1)
         for j in range(begin // 256, end // 256):
-            part = pl.ds(j * 256, 256)
-            d = jnp.dot(pb[j], both, preferred_element_type=F32)
-            sc[s1, part], sc[s2, part] = d[:, :128], d[:, 128:]
-
-    def statistics(begin, end, s1, s2):
-        for s in (s1, s2):
+            d = jnp.dot(pb[j], right, preferred_element_type=F32)
+            for t, s in enumerate(slots):
+                sc[s, j * 256 : (j + 1) * 256] = d[:, t * 128 : (t + 1) * 128]
+
+    def statistics(begin, end, *slots):
+        for s in slots:
             v = sc[s, begin:end].reshape((end - begin) // 8, 8, 128)
             chosen = jnp.zeros((8, 128), F32)
             for j in range(begin // 256, end // 256):
@@ -222,9 +226,6 @@
 
     along(1)
     along(2)
-    for copy in pos_z:
-        copy.wait_recv()
-    lax.fori_loop(0, 16, mask, 0)
     early = [
         (slot(a, b3), slot(a, b1)),
         (slot(a3, b), slot(a1, b)),
@@ -246,19 +247,19 @@
     flip(me)
     landed(0, 1, 3, 4)
     flip(*early[0], *early[1])
-    score((0, 256, *early[0]), (0, 256, *early[1]))
+    score((0, 256, *early[0], *early[1]))
     along(3)
     landed(5, 6, 7, 8)
     flip(*early[2], *early[3])
-    score((0, 256, *early[2]), (0, 256, *early[3]))
+    score((0, 256, *early[2], *early[3]))
     pu1.wait_recv()
     pd1.wait_recv()
     turn(1)
     turn(2)
-    score(*[(256, 768, *pair) for pair in early[:2]])
+    score((256, 768, *early[0], *early[1]))
     last(0)
     last(1)
-    score(*[(256, 768, *pair) for pair in early[2:]])
+    score((256, 768, *early[2], *early[3]))
     last(2)
     landed(2, 11)
     flip(*late[0])
@@ -272,7 +273,8 @@
     score((0, 768, *late[2]))
     pfu.wait_recv()
     pfd.wait_recv()
-    score(*[(768, 1024, *pair) for pair in early + late[:3]])
+    quads = [early[0] + early[1], early[2] + early[3], late[0] + late[1], late[2]]
+    score(*[(768, 1024, *quad) for quad in quads])
     landed(14)
     flip(late[3][1])
     score((0, 1024, *late[3]))
@@ -336,12 +338,14 @@
     a_order, b_order = [a2, a3, a1, a], [b2, b3, b1, b]
 
     def weigh(s, _):
+        wb[:, columns(s)] = (sc[s] * lser[0, pl.ds(s, 1), :]).astype(BF16)
+        return 0
+
+    def weigh_less(s, _):
         row = pl.ds(s, 1)
         for j in range(4):
             part = pl.ds(j * 256, 256)
-            e = sc[s, part]
-            wb[part, columns(s)] = (e * lser[0, row, :]).astype(BF16)
-            less = jnp.where(hits(s, j), lser[4, row, :], e * lser[2, row, :])
+            less = jnp.where(hits(s, j), lser[4, row, :], sc[s, part] * lser[2, row, :])
             wq[part, columns(s)] = less.astype(BF16)
         return 0
 
@@ -397,12 +401,16 @@
         for t, s in enumerate(mine_slots(k)):
             accq[s] += rq[k, t]
 
-    def hop_p(h, n, j, half, device):
-        v, scale = quantized(accp[j, half, h * 256 : (h + 1) * 256])
-        ys[h, n] = v
-        for k in range(2):
-            yss[h, n, k : k + 1, :] = scale[:, k * 128 : (k + 1) * 128]
-        return send(ys.at[h, n], yr.at[h, n], device), send(yss.at[h, n], yrs.at[h, n], device)
+    def hop_p(h, *hops):
+        for n, j, half, _ in hops:
+            v, scale = quantized(accp[j, half, h * 256 : (h + 1) * 256])
+            ys[h, n] = v
+            for k in range(2):
+                yss[h, n, k : k + 1, :] = scale[:, k * 128 : (k + 1) * 128]
+        for n, _, _, device in hops:
+            hops_p[h, n] = (
+                send(ys.at[h, n], yr.at[h, n], device), send(yss.at[h, n], yrs.at[h, n], device)
+            )
 
     def arrive_p(h, n, hop):
         for copy in hop:
@@ -413,28 +421,28 @@
     hops_p = {}
 
     def begin_p(h):
-        hops_p[h, 0] = hop_p(h, 0, 3, lo, y_up)
-        hops_p[h, 1] = hop_p(h, 1, 3, hi, y_down)
-        hops_p[h, 2] = hop_p(h, 2, 2, hi, y_up)
-        hops_p[h, 3] = hop_p(h, 3, 1, lo, y_down)
+        hop_p(h, (0, 3, lo, y_up), (1, 3, hi, y_down), (2, 2, hi, y_up), (3, 1, lo, y_down))
 
     def relay_p(h):
         part = pl.ds(h * 256, 256)
         accp[2, lo, part] += arrive_p(h, 0, hops_p[h, 0])
-        hops_p[h, 4] = hop_p(h, 4, 2, lo, y_up)
         accp[1, hi, part] += arrive_p(h, 1, hops_p[h, 1])
-        hops_p[h, 5] = hop_p(h, 5, 1, hi, y_down)
+        hop_p(h, (4, 2, lo, y_up), (5, 1, hi, y_down))
 
     def end_p(h):
         part = pl.ds(h * 256, 256)
         accp[0, lo, part] += arrive_p(h, 3, hops_p[h, 3]) + arrive_p(h, 4, hops_p[h, 4])
         accp[0, hi, part] += arrive_p(h, 2, hops_p[h, 2]) + arrive_p(h, 5, hops_p[h, 5])
 
-    def hop_b(n, k, side, device):
-        for t, s in enumerate(mine_slots(k)):
-            bs[n, t], scale = quantized(accq[s, halves[side]])
-            bss[n, t : t + 1, :] = scale
-        return send(bs.at[n], br.at[n], device), send(bss.at[n], brs.at[n], device)
+    def hop_b(*hops):
+        for n, k, side, _ in hops:
+            for t, s in enumerate(mine_slots(k)):
+                bs[n, t], scale = quantized(accq[s, halves[side]])
+                bss[n, t : t + 1, :] = scale
+        return [
+            (send(bs.at[n], br.at[n], device), send(bss.at[n], brs.at[n], device))
+            for n, _, _, device in hops
+        ]
 
     def arrive_b(n, hop, k, side):
         for copy in hop:
@@ -442,63 +450,64 @@
         for t, s in enumerate(mine_slots(k)):
             accq[s, halves[side]] += restored(br[n, t], brs[n, t : t + 1, :])
 
-    def hop_a(n, da, side, device):
-        az[n], scale = quantized(accq[slot(da, b), halves[side]])
-        azs[n, 0:1, :] = scale
-        return send(az.at[n], ar.at[n], device), send(azs.at[n], ars.at[n], device)
+    def hop_a(*hops):
+        for n, da, side, _ in hops:
+            az[n], scale = quantized(accq[slot(da, b), halves[side]])
+            azs[n, 0:1, :] = scale
+        return [
+            (send(az.at[n], ar.at[n], device), send(azs.at[n], ars.at[n], device))
+            for n, _, _, device in hops
+        ]
 
     def arrive_a(n, hop, da, side):
         for copy in hop:
             copy.wait_recv()
         accq[slot(da, b), halves[side]] += restored(ar[n], ars[n, 0:1, :])
 
-    lax.fori_loop(0, 16, weigh, 0)
+    lax.fori_loop(0, 16, weigh_less, 0)
     grad_other(0)
     grad_other(1)
     grad_mine(0)
+    lax.fori_loop(0, 16, weigh, 0)
+    swapped(0)
+    qu_a, qd_a = hop_b((0, 0, 0, b_up), (1, 0, 1, b_down))
     grad_p(0)
     begin_p(0)
-    swapped(0)
-    qu_a = hop_b(0, 0, 0, b_up)
-    qd_a = hop_b(1, 0, 1, b_down)
     grad_other(2)
     grad_mine(1)
     swapped(1)
-    qd_b = hop_b(2, 1, 0, b_down)
+    (qd_b,) = hop_b((2, 1, 0, b_down))
     grad_mine(2)
+    grad_other(3)
+    swapped(2)
+    (qu_b,) = hop_b((3, 2, 1, b_up))
     grad_p(1)
     begin_p(1)
-    swapped(2)
-    qu_b = hop_b(3, 2, 1, b_up)
+    arrive_b(0, qu_a, 2, 0)
+    arrive_b(1, qd_a, 1, 1)
+    qu_c, qd_c = hop_b((4, 2, 0, b_up), (5, 1, 1, b_down))
+    relay_p(0)
     grad_p(2)
     begin_p(2)
-    relay_p(0)
-    arrive_b(0, qu_a, 2, 0)
-    qu_c = hop_b(4, 2, 0, b_up)
-    arrive_b(1, qd_a, 1, 1)
-    qd_c = hop_b(5, 1, 1, b_down)
     grad_p(3)
     begin_p(3)
+    grad_mine(3)
     relay_p(1)
-    grad_other(3)
-    grad_mine(3)
+    swapped(3)
     grad_own(0)
-    relay_p(2)
-    swapped(3)
     arrive_b(2, qd_b, 3, 0)
     arrive_b(3, qu_b, 3, 1)
     arrive_b(5, qd_c, 3, 1)
     arrive_b(4, qu_c, 3, 0)
-    vu_a = hop_a(0, a2, 0, a_up)
-    vd_a = hop_a(1, a2, 1, a_down)
-    vd_b = hop_a(2, a3, 0, a_down)
-    vu_b = hop_a(3, a1, 1, a_up)
+    vu_a, vd_a, vd_b, vu_b = hop_a(
+        (0, a2, 0, a_up), (1, a2, 1, a_down), (2, a3, 0, a_down), (3, a1, 1, a_up)
+    )
+    relay_p(2)
+    arrive_a(0, vu_a, a1, 0)
+    arrive_a(1, vd_a, a3, 1)
+    vu_c, vd_c = hop_a((4, a1, 0, a_up), (5, a3, 1, a_down))
     relay_p(3)
     grad_own(1)
-    arrive_a(0, vu_a, a1, 0)
-    vu_c = hop_a(4, a1, 0, a_up)
-    arrive_a(1, vd_a, a3, 1)
-    vd_c = hop_a(5, a3, 1, a_down)
     grad_own(2)
     arrive_a(2, vd_b, a, 0)
     arrive_a(3, vu_b, a, 1)
@@ -529,8 +538,9 @@
     copy.start()
     left.append(copy)
     loss_copy.wait_recv()
-    loss_ref[0:1, :] = lossb[0, 0:1, :]
-    loss_ref[1:2, :] = lossb[1, 0:1, :]
+    copy = pltpu.make_async_copy(lossb, loss_ref, lsem.at[5])
+    copy.start()
+    left.append(copy)
     for copy in out1:
         copy.wait_recv()
     out3 = share(1 - y_lo, partner)
@@ -541,7 +551,9 @@
     for copy in out3:
         copy.wait_recv()
     leave(1 - y_lo, 1 - c, 4)
-    fins_ref[...] = fins[...]
+    copy = pltpu.make_async_copy(fins, fins_ref, lsem.at[6])
+    copy.start()
+    left.append(copy)
     for copy in left:
         copy.wait()
     for k, copy in enumerate(started):
@@ -554,23 +566,23 @@
         scale = jnp.concatenate([fins_ref[0, core, k : k + 1, :] for k in range(4)], axis=1)
         gq_out[:, core * 512 : (core + 1) * 512] = restored(fin_ref[0, core], scale)
     gp_out[...] = gp_ref[...]
-    loss_out[...] = loss_ref[...]
+    for h in range(2):
+        loss_out[h : h + 1, :] = loss_ref[h, 0:1, :]
 
 
 def local(queries, passages, positive):
     vmem = pltpu.VMEM
-    space = pl.BlockSpec(memory_space=vmem)
     anywhere = pl.BlockSpec(memory_space=pl.ANY)
     loss, fin, fins, gp = pl.pallas_call(
         kernel,
         out_shape=(
-            jax.ShapeDtypeStruct((2, 128), F32),
+            jax.ShapeDtypeStruct((2, 8, 128), F32),
             jax.ShapeDtypeStruct((2, 2, 128, 512), I16),
             jax.ShapeDtypeStruct((2, 2, 4, 128), F32),
             jax.ShapeDtypeStruct((256, 1024), F32),
         ),
-        in_specs=[anywhere, anywhere, space],
-        out_specs=(space, anywhere, space, anywhere),
+        in_specs=[anywhere] * 3,
+        out_specs=(anywhere,) * 4,
         scratch_shapes=[
             vmem((16, 128, 1024), BF16),
             vmem((1024, 2048), BF16),
@@ -582,6 +594,7 @@
             vmem((1024, 2048), BF16),
             vmem((16, 512, 128), F32),
             vmem((4, 256, 1024), F32),
+            vmem((2, 128), jnp.int32),
             vmem((4, 4, 8, 128), jnp.int32),
             vmem((3, 16, 8, 128), F32),
             vmem((2, 16, 128), F32),
@@ -606,7 +619,7 @@
             vmem((2, 2, 128, 512), I16),
             vmem((2, 2, 4, 128), F32),
             vmem((2, 8, 128), F32),
-            pltpu.SemaphoreType.DMA((5,)),
+            pltpu.SemaphoreType.DMA((7,)),
             pltpu.SemaphoreType.DMA((SENDS,)),
             pltpu.SemaphoreType.DMA((RECEIVES,)),
         ],
@@ -626,7 +639,7 @@
             pl.BlockSpec((1, 2, 128, 512), lambda h: (h, 0, 0, 0)),
             pl.BlockSpec((1, 2, 4, 128), lambda h: (h, 0, 0, 0)),
             pl.BlockSpec((128, 1024), lambda h: (h, 0)),
-            pl.BlockSpec((2, 128), lambda h: (0, 0)),
+            pl.BlockSpec((2, 8, 128), lambda h: (0, 0, 0)),
         ],
         out_specs=(
             pl.BlockSpec((128, 1024), lambda h: (h, 0)),

time: 78.6 us -> 77.7 us (0.989)
  Pallas kernels: 77.8 us -> 76.9 us
    pallas_call x1, Pallas kernels: 75.3 us -> 74.4 us  [local(): pl.pallas_call(kernel, out_shape=(jax.ShapeDtypeStruct((2, 8, 128), F32),...]
where the time goes in v5:
time: 77.7 us; the launch traced here: 77.6 us
  Pallas kernels  76.9 us (99%)
    pallas_call x1, Pallas kernels, local(): pl.pallas_call(kernel, out_shape=(jax.ShapeDtypeStruct((2, 8, 128), F32),...  74.4 us
    pallas_call x1, Pallas kernels, local(): pl.pallas_call(finish, grid=(2,), out_shape=(jax.ShapeDtypeStruct((256, 1...  2.53 us

profile of v5, /device:TPU:1, one launch (start us, length us, event | category | flops | bytes accessed | tf_op | source)
XLA Modules:
  0.0 77.6 jit_solution(2007591726442437261)
XLA Ops:
  0.6 74.4 %shard_map.58 = (f32[2,8,128]{2,1,0:T(8,128)}, s16[2,2,128,512]{3,2,1,0:T(8,128)(2,1)}, f32[2,2,4,128]{3,2,1,0:T(4,128)}, f32[256,1024]{1,0:T(8,128)}) custom-call(bf16[256,1024]{1,0:T(8,128)(2,1)} %q_ref.1, bf16[256,1024]{1,0:T(8,128)(2,1)} %p_ref.1, s32[2,128]{1,0:T(2,128)} %bitcast.2), custom_call_target="tpu_custom_call" | custom-call | tf_op jit(solution)/shard_map/pallas_call | solution.py:576
  75.0 2.5 %shard_map.59 = (f32[256,1024]{1,0:T(8,128)}, f32[256,1024]{1,0:T(8,128)}, f32[2,128]{1,0:T(2,128)}) custom-call(s16[2,2,128,512]{3,2,1,0:T(8,128)(2,1)} %get-tuple-element.10.fin_ref, f32[2,2,4,128]{3,2,1,0:T(4,128)} %get-tuple-element.11.fins_ref, f32[256,1024]{1,0:T(8,128)} %get-tuple-element.12.gp_ref, f32[2,8,128]{2,1,0:T(8,128)} %get-tuple-element.13.loss_ref), custom_call_target="tpu_custom_call" | custom-call | tf_op jit(solution)/shard_map/pallas_call | solution.py:630
